TPU v7x, 32 devices: a whole 2x2x4 slice. The times are simulated.
32 devices in a mesh: gx: 4 (over z), gy: 4 (over y, x), gz: 2 (over core).
Axes of the slice: x: 2, y: 2, z: 4, core: 2. Of those that a mesh axis runs over, the one named last changes fastest.
Arguments:
- chi_field: float32 [32, 128, 256], P('gx', 'gy', 'gz'), may hold values from 0.5 to 2.5, as said below
- metric: float32 [6, 32, 128, 256], P(None, 'gx', 'gy', 'gz'), may hold values from -0.3 to 1.5, as said below
- curvature: float32 [6, 32, 128, 256], P(None, 'gx', 'gy', 'gz'), may hold values from -1.6 to 1.6
- trace_curvature: float32 [32, 128, 256], P('gx', 'gy', 'gz'), may hold values from -3 to 3
- gamma_field: float32 [3, 32, 128, 256], P(None, 'gx', 'gy', 'gz'), may hold values from -1.6 to 1.6
Outputs:
- hamiltonian: float32 [32, 128, 256], P('gx', 'gy', 'gz')
- momentum: float32 [3, 32, 128, 256], P(None, 'gx', 'gy', 'gz')
- constraint_norms: float32 [2], replicated
Inputs may be any that keep to these rules, and one draw needn't show every extreme that they name: `chi_field`: positive. `metric`: at every cell the symmetric 3x3 matrix built from the six components is positive definite with a dominant diagonal.
All inputs are finite; a program needn't handle non-finite values.
Results may differ from a plain program's by a relative error of at most 0.0003.
Values sent between devices are 32-bit elements; how exact they have to be, the bound alone decides.
A program may use at most 128 MiB of HBM per device.

v0:
```python
import functools

import jax
import jax.numpy as jnp
import numpy as np
from jax import lax
from jax.experimental import pallas as pl
from jax.experimental.pallas import tpu as pltpu
from jax.sharding import PartitionSpec as P

pair_index = ((0, 1, 2), (1, 3, 4), (2, 4, 5))
MESH = pl.DeviceIdType.MESH
CHI, MET, CURV, TRK, GX, GY, GZ = 0, 1, 7, 13, 14, 15, 16
GEO = 7
Z_FIELDS = tuple(range(14)) + (GZ,)
TOP = 8


def first(m2, m1, p1, p2):
    return 8.0 * (p1 - m1) - (p2 - m2)


def second(m2, m1, c, p1, p2):
    return 16.0 * (p1 + m1) - (p2 + m2) - 30.0 * c


def total_of(terms):
    terms = list(terms)
    while len(terms) > 1:
        terms = [
            terms[n] + terms[n + 1] if n + 1 < len(terms) else terms[n]
            for n in range(0, len(terms), 2)
        ]
    return terms[0]


def sym(values, i, j):
    return values[pair_index[i][j]]


def contract(gu, values):
    return total_of(
        [gu[n] * values[n] for n in (0, 3, 5)]
        + [2.0 * total_of(gu[n] * values[n] for n in (1, 2, 4))]
    )


def z_weights():
    weights = np.zeros((len(Z_FIELDS), 256, 256), np.float32)
    for n in range(len(Z_FIELDS)):
        for z in range(128):
            for step, one, two in ((-2, 1, -1), (-1, -8, 16), (0, 0, -30), (1, 8, 16), (2, -1, -1)):
                at = z + step
                row = at if 0 <= at < 128 else 128 + 4 * n + (at + 2 if at < 0 else at - 126)
                weights[n, row, z] = one
                weights[n, row, 128 + z] = two
    return weights


def split(value):
    high = value.astype(jnp.bfloat16)
    return high, (value - high.astype(jnp.float32)).astype(jnp.bfloat16)


def along_z(value, packed, weights):
    parts = [jnp.concatenate([a, b], 1) for a, b in zip(split(value), split(packed))]
    return sum(jnp.dot(part, weights, preferred_element_type=jnp.float32) for part in parts)


def inverse(metric):
    g00, g01, g02, g11, g12, g22 = metric
    m00 = g11 * g22 - g12 * g12
    m01 = g02 * g12 - g01 * g22
    m02 = g01 * g12 - g02 * g11
    m11 = g00 * g22 - g02 * g02
    m12 = g01 * g02 - g00 * g12
    m22 = g00 * g11 - g01 * g01
    scale = 1.0 / (g00 * m00 + g01 * m01 + g02 * m02)
    return [m * scale for m in (m00, m01, m02, m11, m12, m22)]


def cell_math(load, load_dx, load_dy, load_z, load_zz, load_xz, load_yz, load_part):
    zpos = {f: n for n, f in enumerate(Z_FIELDS)}
    gu = inverse([load(MET + n, 0, 0) for n in range(6)])
    gu_hess = [12.0 * gu[n] if n in (0, 3, 5) else 2.0 * gu[n] for n in range(6)]

    def geo(f):
        c = load(f, 0, 0)
        xs = [load(f, s, 0) for s in (-2, -1, 1, 2)]
        ys = [load(f, 0, s) for s in (-2, -1, 1, 2)]
        dx = load_dx(f, 0)
        dy, dz = load_dy(f), load_z(f)
        dxx = second(xs[0], xs[1], c, xs[2], xs[3])
        dyy = second(ys[0], ys[1], c, ys[2], ys[3])
        dzz = load_zz(f)
        dxy = first(*(load_dx(f, s) for s in (-2, -1, 1, 2)))
        dxz, dyz = load_xz(f), load_yz(f)
        hess = (dxx, dxy, dxz, dyy, dyz, dzz)
        return (dx, dy, dz), total_of(gu_hess[n] * hess[n] for n in range(6))

    chi = load(CHI, 0, 0)
    dchi, chi_box = geo(CHI)
    grads = [[None] * 6 for _ in range(3)]
    boxes = []
    for n in range(6):
        d, box = geo(MET + n)
        for a in range(3):
            grads[a][n] = d[a]
        boxes.append(box)
    metric_box = contract(gu, boxes)

    raised = [
        [[total_of(sym(gu, b, l) * sym(grads[k], l, j) for l in range(3)) for j in range(3)] for b in range(3)]
        for k in range(3)
    ]
    trace = [raised[k][0][0] + raised[k][1][1] + raised[k][2][2] for k in range(3)]
    lower = [
        raised[0][0][l] + raised[1][1][l] + raised[2][2][l] - 0.5 * trace[l] for l in range(3)
    ]
    gd = [total_of(sym(gu, k, l) * lower[l] for l in range(3)) for k in range(3)]

    def trace_of(k, l):
        return total_of(raised[k][a][b] * raised[l][b][a] for a in range(3) for b in range(3))

    square = contract(gu, [trace_of(k, l) for k in range(3) for l in range(k, 3)])

    def cross_of(k, b):
        left, right = raised[k][b], raised[b][k]
        up = [total_of(sym(gu, c, j) * right[j] for j in range(3)) for c in range(3)]
        return total_of(left[c] * up[c] for c in range(3))

    cross = (
        cross_of(0, 0)
        + cross_of(1, 1)
        + cross_of(2, 2)
        + 2.0 * (cross_of(0, 1) + cross_of(0, 2) + cross_of(1, 2))
    )
    chi_up = [total_of(sym(gu, k, l) * dchi[l] for l in range(3)) for k in range(3)]
    grad_sq = total_of(chi_up[k] * dchi[k] for k in range(3))
    laplace = chi_box - total_of(gd[k] * dchi[k] for k in range(3))
    drift = total_of(gd[k] * trace[k] for k in range(3))

    def dx_of(f):
        return first(*(load(f, s, 0) for s in (-2, -1, 1, 2)))

    def dy_of(f):
        return first(*(load(f, 0, s) for s in (-2, -1, 1, 2)))

    def dz_of(f):
        return load_z(zpos[f])

    div = dx_of(GX) + dy_of(GY) + dz_of(GZ)
    inv_chi = 1.0 / chi
    curv = [load(CURV + n, 0, 0) for n in range(6)]
    mixed = [
        [total_of(sym(curv, i, k) * sym(gu, k, j) for k in range(3)) for j in range(3)] for i in range(3)
    ]
    curv_up = [
        total_of(sym(gu, i, a) * mixed[a][j] for a in range(3)) for i in range(3) for j in range(i, 3)
    ]
    curv_sq = contract(curv, curv_up)
    trk = load(TRK, 0, 0)
    ham = (
        chi * ((0.25 * square + 0.5 * (cross + drift - metric_box)) * (1.0 / 144.0) + div * (1.0 / 12.0))
        + (2.0 * laplace - 2.5 * grad_sq * inv_chi) * (1.0 / 144.0)
        + (2.0 / 3.0) * trk * trk
        - curv_sq
    )
    push = [gd[l] + 1.5 * inv_chi * chi_up[l] for l in range(3)]
    curv_grads = [[op(CURV + n) for n in range(6)] for op in (dx_of, dy_of, dz_of)]
    trace_grads = [op(TRK) for op in (dx_of, dy_of, dz_of)]
    momentum = []
    for i in range(3):
        parts = total_of(sym(gu, j, k) * sym(curv_grads[j], k, i) for j in range(3) for k in range(3))
        parts = parts + load_part(i)
        parts = parts - total_of(sym(curv, l, i) * push[l] for l in range(3))
        parts = parts - 0.5 * contract(curv_up, grads[i]) - (2.0 / 3.0) * trace_grads[i]
        momentum.append(parts * (1.0 / 12.0))
    return ham, momentum


def kernel(
    sizes,
    chi_in, met_in, curv_in, trk_in, gam_in, weights_in,
    ham_out, mom_out, norm_out,
    cells, packed, pack_own, pack_left, pack_right, slope, sums,
    part_out, part, weights, z_one, z_two, y_one, yz_two, xz_two,
    slots_x, slots_y,
    load_sem, xs, xr, ys, yr, zs, zr, es, er, pxs, pxr, pys, pyr,
    rxs, rxr, rys, ryr, cs, cr,
):
    nx, ny, nz = sizes
    cx, cy = chi_in.shape[0], chi_in.shape[1]
    names = ("gx", "gy", "gz")
    me = [lax.axis_index(a) for a in names]

    def moved(axis, step):
        return lax.rem(me[axis] + step + sizes[axis], sizes[axis])

    def peer(axes, steps):
        where = list(me)
        if isinstance(axes, int):
            axes, steps = (axes,), (steps,)
        for axis, step in zip(axes, steps):
            where[axis] = moved(axis, step)
        return tuple(where)

    def hops(axes):
        return [step for step in np.ndindex(*(sizes[a] for a in axes)) if any(step)]

    def place_in(axes, steps=None):
        index = 0
        for axis, step in zip(axes, steps or (0,) * len(axes)):
            index = index * sizes[axis] + moved(axis, step)
        return index

    own_x, own_y = pl.ds(2, cx), pl.ds(TOP, cy)
    loads = [
        pltpu.make_async_copy(src, dst, load_sem.at[n])
        for n, (src, dst) in enumerate(
            (
                (chi_in, cells.at[CHI, own_x, own_y]),
                (met_in, cells.at[pl.ds(MET, 6), own_x, own_y]),
                (curv_in, cells.at[pl.ds(CURV, 6), own_x, own_y]),
                (trk_in, cells.at[TRK, own_x, own_y]),
                (gam_in, cells.at[pl.ds(GX, 3), own_x, own_y]),
                (weights_in, weights),
            )
        )
    ]
    for copy in loads:
        copy.start()
    barrier = pltpu.get_barrier_semaphore()
    for axes in ((1, 2), (0,)):
        for step in hops(axes):
            pl.semaphore_signal(barrier, inc=1, device_id=peer(axes, step), device_id_type=MESH)
    pl.semaphore_wait(barrier, ny * nz + nx - 2)

    def send(src, dst, send_sem, recv_sem, axis, step):
        copy = pltpu.make_async_remote_copy(
            src_ref=src, dst_ref=dst, send_sem=send_sem, recv_sem=recv_sem,
            device_id=peer(axis, step), device_id_type=MESH,
        )
        copy.start()
        return copy

    for copy in loads[:5]:
        copy.wait()
    low_x, high_x = pl.ds(2, 2), pl.ds(cx, 2)
    x_faces = []
    for n, fields in enumerate((pl.ds(0, GEO), pl.ds(GX, 1))):
        x_faces += [
            send(cells.at[fields, high_x, own_y], cells.at[fields, pl.ds(0, 2), own_y], xs.at[2 * n], xr.at[2 * n], 0, 1),
            send(cells.at[fields, low_x, own_y], cells.at[fields, pl.ds(cx + 2, 2), own_y], xs.at[2 * n + 1], xr.at[2 * n + 1], 0, -1),
        ]
    low_y, high_y = pl.ds(TOP, 2), pl.ds(TOP + cy - 2, 2)
    before_y, after_y = pl.ds(TOP - 2, 2), pl.ds(TOP + cy, 2)
    y_faces = [
        send(cells.at[pl.ds(0, 16), own_x, high_y], cells.at[pl.ds(0, 16), own_x, before_y], ys.at[0], yr.at[0], 1, 1),
        send(cells.at[pl.ds(0, 16), own_x, low_y], cells.at[pl.ds(0, 16), own_x, after_y], ys.at[1], yr.at[1], 1, -1),
    ]
    tiles = cy // 8
    lane = lax.broadcasted_iota(jnp.int32, (8, 128), 1)

    def pack(step, carry):
        x, y = step // tiles, lax.rem(step, tiles) * 8
        rows = pl.ds(pl.multiple_of(TOP + y, 8), 8)
        value = jnp.zeros((8, 128), jnp.float32)
        group = lax.shift_right_logical(lane, 2)
        for n, f in enumerate(Z_FIELDS):
            value = jnp.where(group == n, pltpu.roll(cells[f, x + 2, rows], 4 * n + 2, 1), value)
        pack_own[x, pl.ds(pl.multiple_of(y, 8), 8)] = value
        return carry

    lax.fori_loop(0, cx * tiles, pack, 0)
    z_faces = [
        send(pack_own, pack_left, zs.at[0], zr.at[0], 2, 1),
        send(pack_own, pack_right, zs.at[1], zr.at[1], 2, -1),
    ]
    for copy in z_faces:
        copy.wait_recv()

    def merge(x, carry):
        wide = lax.broadcasted_iota(jnp.int32, (cy, 128), 1)
        packed[x + 2, own_y] = jnp.where((wide & 2) == 0, pack_left[x], pack_right[x])
        return carry

    lax.fori_loop(0, cx, merge, 0)
    px_faces = [
        send(packed.at[high_x, own_y], packed.at[pl.ds(0, 2), own_y], pxs.at[0], pxr.at[0], 0, 1),
        send(packed.at[low_x, own_y], packed.at[pl.ds(cx + 2, 2), own_y], pxs.at[1], pxr.at[1], 0, -1),
    ]
    py_faces = [
        send(packed.at[own_x, high_y], packed.at[own_x, before_y], pys.at[0], pyr.at[0], 1, 1),
        send(packed.at[own_x, low_y], packed.at[own_x, after_y], pys.at[1], pyr.at[1], 1, -1),
    ]
    edges = []
    for n, rows in enumerate((before_y, after_y)):
        y_faces[n].wait_recv()
        edges += [
            send(cells.at[pl.ds(0, GEO), high_x, rows], cells.at[pl.ds(0, GEO), pl.ds(0, 2), rows], es.at[2 * n], er.at[2 * n], 0, 1),
            send(cells.at[pl.ds(0, GEO), low_x, rows], cells.at[pl.ds(0, GEO), pl.ds(cx + 2, 2), rows], es.at[2 * n + 1], er.at[2 * n + 1], 0, -1),
        ]
    for copy in py_faces:
        copy.wait_recv()

    sums[...] = jnp.zeros_like(sums)
    loads[5].wait()
    flat = (cx * cy, 128)

    def geo_z(f, carry):
        mid = packed[own_x, own_y].reshape(flat)
        both = along_z(cells[f, own_x, own_y].reshape(flat), mid, weights[f])
        z_one[f] = both[:, :128].reshape(cx, cy, 128)
        z_two[f] = both[:, 128:].reshape(cx, cy, 128)
        dy = first(*(cells[f, own_x, pl.ds(TOP + s, cy)] for s in (-2, -1, 1, 2)))
        dy_packed = first(*(packed[own_x, pl.ds(TOP + s, cy)] for s in (-2, -1, 1, 2)))
        y_one[f] = dy
        yz_two[f] = along_z(dy.reshape(flat), dy_packed.reshape(flat), weights[f, :, :128]).reshape(cx, cy, 128)
        return carry

    lax.fori_loop(0, GEO, geo_z, 0)

    def rest_z(n, carry):
        f = jnp.where(n == 14, GZ, n)
        mid = packed[own_x, own_y].reshape(flat)
        z_one[n] = along_z(cells[f, own_x, own_y].reshape(flat), mid, weights[n, :, :128]).reshape(cx, cy, 128)
        return carry

    lax.fori_loop(GEO, len(Z_FIELDS), rest_z, 0)

    part[:, pl.ds(2, cx - 4)] = jnp.zeros((3, cx - 4, cy, 128), jnp.float32)
    missing = jnp.zeros((7, 2, cy, 128), jnp.float32)
    cells[pl.ds(CURV, 7), pl.ds(0, 2), own_y] = missing
    cells[pl.ds(CURV, 7), pl.ds(cx + 2, 2), own_y] = missing
    x_faces[0].wait_recv()
    x_faces[1].wait_recv()

    def offer(t, carry):
        rows = pl.ds(pl.multiple_of(TOP + t * 8, 8), 8)
        out_rows = pl.ds(pl.multiple_of(t * 8, 8), 8)
        for side, far, near, at, behind, sign in ((0, 0, 1, 2, 3, 1.0), (1, cx + 3, cx + 2, cx + 1, cx, -1.0)):
            edge = [cells[CURV + n, at, rows] * sign for n in range(7)]
            second_edge = [cells[CURV + n, behind, rows] * sign for n in range(7)]
            for place, slot, values in (
                (near, 1 - side, [8.0 * a - b for a, b in zip(edge, second_edge)]),
                (far, side, [-a for a in edge]),
            ):
                gu = inverse([cells[MET + n, place, rows] for n in range(6)])
                for i in range(3):
                    value = total_of(sym(gu, 0, k) * sym(values, k, i) for k in range(3))
                    if i == 0:
                        value = value - (2.0 / 3.0) * values[6]
                    part_out[side, i, slot, out_rows] = value
        return carry

    lax.fori_loop(0, tiles, offer, 0)
    part_faces = [
        send(part_out.at[0], part.at[:, pl.ds(cx - 2, 2)], cs.at[0], cr.at[0], 0, -1),
        send(part_out.at[1], part.at[:, pl.ds(0, 2)], cs.at[1], cr.at[1], 0, 1),
    ]

    def group(step, carry):
        base = lax.rem(2 * step + 2, cx)

        @pl.when(2 * step == cx - 4)
        def _():
            for copy in x_faces[2:] + px_faces + edges + part_faces:
                copy.wait_recv()

        def slopes(f, inner):
            slope[f] = first(*(cells[f, pl.ds(base + 2 + s, 2)] for s in (-2, -1, 1, 2)))
            dx = slope[f, :, own_y].reshape(2 * cy, 128)
            dx_packed = first(*(packed[pl.ds(base + 2 + s, 2), own_y] for s in (-2, -1, 1, 2)))
            xz_two[f] = along_z(dx, dx_packed.reshape(2 * cy, 128), weights[f, :, :128]).reshape(2, cy, 128)
            return inner

        lax.fori_loop(0, GEO, slopes, 0)

        def tile(n, inner):
            half, y = n // tiles, lax.rem(n, tiles) * 8
            x = base + half
            rows = pl.ds(pl.multiple_of(y, 8), 8)
            ham, momentum = cell_math(
                lambda f, sx, sy: cells[f, x + 2 + sx, pl.ds(TOP + y + sy, 8)],
                lambda f, sy: slope[f, half, pl.ds(TOP + y + sy, 8)],
                lambda f: y_one[f, x, rows],
                lambda f: z_one[f, x, rows],
                lambda f: z_two[f, x, rows],
                lambda f: xz_two[f, half, rows],
                lambda f: yz_two[f, x, rows],
                lambda i: part[i, x, rows],
            )
            ham_out[x, rows] = ham
            for i in range(3):
                mom_out[i, x, rows] = momentum[i]
            sums[0] += ham * ham
            sums[1] += momentum[0] * momentum[0] + momentum[1] * momentum[1] + momentum[2] * momentum[2]
            return inner

        lax.fori_loop(0, 2 * tiles, tile, 0)
        return carry

    lax.fori_loop(0, cx // 2, group, 0)

    row = lax.broadcasted_iota(jnp.int32, (8, 128), 0)
    ham_sum = jnp.sum(sums[0], axis=0, keepdims=True)
    mom_sum = jnp.sum(sums[1], axis=0, keepdims=True)
    total = jnp.where(row == 0, ham_sum, jnp.where(row == 1, mom_sum, 0.0))
    pending = []
    for axes, slots, ss, rs in (((1, 2), slots_y, rys, ryr), ((0,), slots_x, rxs, rxr)):
        here = place_in(axes)
        slots[here] = total
        others = hops(axes)
        for n, step in enumerate(others):
            pending.append(send(slots.at[here], slots.at[here], ss.at[n], rs.at[here], axes, step))
        for n, step in enumerate(others):
            source = place_in(axes, step)
            pltpu.make_async_remote_copy(
                src_ref=slots.at[source], dst_ref=slots.at[source], send_sem=ss.at[n],
                recv_sem=rs.at[source], device_id=peer(axes, step), device_id_type=MESH,
            ).wait_recv()
        total = total_of(slots[n] for n in range(len(others) + 1))
    count = float(cx * cy * 128 * nx * ny * nz)
    rates = jnp.where(row == 0, 1.0 / count, 1.0 / (3.0 * count))
    root = jnp.sqrt(jnp.sum(total, axis=1, keepdims=True) * rates)
    norm_out[0] = root[0, 0]
    norm_out[1] = root[1, 0]
    for copy in x_faces + y_faces + z_faces + px_faces + py_faces + edges + part_faces + pending:
        copy.wait_send()


def on_device(chi_field, metric, curvature, trace_curvature, gamma_field):
    sizes = tuple(lax.axis_size(a) for a in ("gx", "gy", "gz"))
    cx, cy, cz = chi_field.shape
    dma = pltpu.SemaphoreType.DMA
    vmem = pl.BlockSpec(memory_space=pltpu.VMEM)
    block = (cx + 4, cy + 2 * TOP, cz)
    return pl.pallas_call(
        functools.partial(kernel, sizes),
        out_shape=(
            jax.ShapeDtypeStruct(chi_field.shape, jnp.float32),
            jax.ShapeDtypeStruct(gamma_field.shape, jnp.float32),
            jax.ShapeDtypeStruct((2,), jnp.float32),
        ),
        in_specs=[pl.BlockSpec(memory_space=pl.ANY)] * 6,
        out_specs=(vmem, vmem, pl.BlockSpec(memory_space=pltpu.SMEM)),
        scratch_shapes=[
            pltpu.VMEM((17,) + block, jnp.float32),
            pltpu.VMEM(block, jnp.float32),
            pltpu.VMEM((cx, cy, cz), jnp.float32),
            pltpu.VMEM((cx, cy, cz), jnp.float32),
            pltpu.VMEM((cx, cy, cz), jnp.float32),
            pltpu.VMEM((GEO, 2) + block[1:], jnp.float32),
            pltpu.VMEM((2, 8, 128), jnp.float32),
            pltpu.VMEM((2, 3, 2, cy, cz), jnp.float32),
            pltpu.VMEM((3, cx, cy, cz), jnp.float32),
            pltpu.VMEM((len(Z_FIELDS), 256, 256), jnp.bfloat16),
            pltpu.VMEM((len(Z_FIELDS), cx, cy, cz), jnp.float32),
            pltpu.VMEM((GEO, cx, cy, cz), jnp.float32),
            pltpu.VMEM((GEO, cx, cy, cz), jnp.float32),
            pltpu.VMEM((GEO, cx, cy, cz), jnp.float32),
            pltpu.VMEM((GEO, 2, cy, cz), jnp.float32),
        ]
        + [pltpu.VMEM((n, 8, 128), jnp.float32) for n in (sizes[0], sizes[1] * sizes[2])]
        + [dma((6,)), dma((4,)), dma((4,)), dma((2,)), dma((2,)), dma((2,)), dma((2,))]
        + [dma((4,)), dma((4,)), dma((2,)), dma((2,)), dma((2,)), dma((2,))]
        + [dma((n,)) for n in (sizes[0], sizes[1] * sizes[2], 2) for _ in range(2)],
        compiler_params=pltpu.CompilerParams(
            collective_id=0, has_side_effects=True, vmem_limit_bytes=67043328
        ),
    )(chi_field, metric, curvature, trace_curvature, gamma_field, jnp.asarray(z_weights(), jnp.bfloat16))


def solution(mesh):
    return jax.shard_map(
        on_device,
        mesh=mesh,
        in_specs=(
            P("gx", "gy", "gz"),
            P(None, "gx", "gy", "gz"),
            P(None, "gx", "gy", "gz"),
            P("gx", "gy", "gz"),
            P(None, "gx", "gy", "gz"),
        ),
        out_specs=(P("gx", "gy", "gz"), P(None, "gx", "gy", "gz"), P()),
        check_vma=False,
    )
```

profile of v0, /device:TPU:0, one launch (start us, length us, event | category | flops | bytes accessed | tf_op | source)
XLA Modules:
  0.0 43.5 jit_solution(10382726411250079926)
XLA Ops:
  0.6 38.5 %shard_map.85 = (f32[8,32,128]{2,1,0:T(8,128)}, f32[3,8,32,128]{3,2,1,0:T(8,128)}, f32[2]{0:T(128)}) custom-call(f32[8,32,128]{2,1,0:T(8,128)} %chi_in.1, f32[6,8,32,128]{3,2,1,0:T(8,128)} %met_in.1, f32[6,8,32,128]{3,2,1,0:T(8,128)} %curv_in.1, f32[8,32,128]{2,1,0:T(8,128)} %trk_in.1, f32[3,8,32,128]{3,2,1,0:T(8,128)} %gam_in.1, ...), custom_call_target="tpu_custom_call" | custom-call | tf_op jit(solution)/shard_map/pallas_call | solution.py:439
  39.1 1.6 %copy.12 = f32[8,32,128]{2,1,0:T(8,128)} copy(f32[8,32,128]{2,1,0:T(8,128)} %get-tuple-element.6) | data formatting | bytes 262144
  40.7 1.8 %copy.13 = f32[3,8,32,128]{3,2,1,0:T(8,128)} copy(f32[3,8,32,128]{3,2,1,0:T(8,128)} %get-tuple-element.7) | data formatting | bytes 786432
  42.4 1.1 %copy.14 = f32[2]{0:T(128)} copy(f32[2]{0:T(128)} %get-tuple-element.8) | data formatting | bytes 16
where the time goes:
time: 43.7 us; the launch traced here: 43.5 us
  Pallas kernels  38.5 us (88%)
  local copies, waits for them, and re-layouts  4.44 us (10%)
  between operations  0.64 us (1%)
    pallas_call x1, Pallas kernels, on_device(): pl.pallas_call(functools.partial(kernel, sizes), out_shape=(jax.ShapeDtyp...  38.5 us
    unnamed x3, local copies, waits for them, and re-layouts  4.44 us

commit v1 on v0

--- a/solution.py
+++ b/solution.py
@@ -182,7 +182,7 @@
 def kernel(
     sizes,
     chi_in, met_in, curv_in, trk_in, gam_in, weights_in,
-    ham_out, mom_out, norm_out,
+    ham_out, mom_out, total_out,
     cells, packed, pack_own, pack_left, pack_right, slope, sums,
     part_out, part, weights, z_one, z_two, y_one, yz_two, xz_two,
     slots_x, slots_y,
@@ -421,13 +421,27 @@
                 recv_sem=rs.at[source], device_id=peer(axes, step), device_id_type=MESH,
             ).wait_recv()
         total = total_of(slots[n] for n in range(len(others) + 1))
-    count = float(cx * cy * 128 * nx * ny * nz)
-    rates = jnp.where(row == 0, 1.0 / count, 1.0 / (3.0 * count))
-    root = jnp.sqrt(jnp.sum(total, axis=1, keepdims=True) * rates)
-    norm_out[0] = root[0, 0]
-    norm_out[1] = root[1, 0]
+    total_out[...] = total
     for copy in x_faces + y_faces + z_faces + px_faces + py_faces + edges + part_faces + pending:
         copy.wait_send()
+
+
+def deliver(count, ham_in, mom_in, total_in, ham_out, mom_out, norm_out, norm, sems):
+    copies = [
+        pltpu.make_async_copy(mom_in, mom_out, sems.at[0]),
+        pltpu.make_async_copy(ham_in, ham_out, sems.at[1]),
+    ]
+    for copy in copies:
+        copy.start()
+    row = lax.broadcasted_iota(jnp.int32, (8, 128), 0)
+    rates = jnp.where(row == 0, 1.0 / count, 1.0 / (3.0 * count))
+    root = jnp.sqrt(jnp.sum(total_in[...] * rates, axis=1, keepdims=True))
+    norm[0] = root[0, 0]
+    norm[1] = root[1, 0]
+    copies.append(pltpu.make_async_copy(norm, norm_out, sems.at[2]))
+    copies[2].start()
+    for copy in copies:
+        copy.wait()
 
 
 def on_device(chi_field, metric, curvature, trace_curvature, gamma_field):
@@ -436,15 +450,16 @@
     dma = pltpu.SemaphoreType.DMA
     vmem = pl.BlockSpec(memory_space=pltpu.VMEM)
     block = (cx + 4, cy + 2 * TOP, cz)
-    return pl.pallas_call(
+    hbm = pl.BlockSpec(memory_space=pltpu.HBM)
+    ham, momentum, total = pl.pallas_call(
         functools.partial(kernel, sizes),
         out_shape=(
-            jax.ShapeDtypeStruct(chi_field.shape, jnp.float32),
-            jax.ShapeDtypeStruct(gamma_field.shape, jnp.float32),
-            jax.ShapeDtypeStruct((2,), jnp.float32),
+            pltpu.VMEM(chi_field.shape, jnp.float32),
+            pltpu.VMEM(gamma_field.shape, jnp.float32),
+            pltpu.VMEM((8, 128), jnp.float32),
         ),
-        in_specs=[pl.BlockSpec(memory_space=pl.ANY)] * 6,
-        out_specs=(vmem, vmem, pl.BlockSpec(memory_space=pltpu.SMEM)),
+        in_specs=[pl.BlockSpec(memory_space=pltpu.HBM)] * 6,
+        out_specs=(vmem, vmem, vmem),
         scratch_shapes=[
             pltpu.VMEM((17,) + block, jnp.float32),
             pltpu.VMEM(block, jnp.float32),
@@ -467,9 +482,21 @@
         + [dma((4,)), dma((4,)), dma((2,)), dma((2,)), dma((2,)), dma((2,))]
         + [dma((n,)) for n in (sizes[0], sizes[1] * sizes[2], 2) for _ in range(2)],
         compiler_params=pltpu.CompilerParams(
-            collective_id=0, has_side_effects=True, vmem_limit_bytes=67043328
+            collective_id=0, has_side_effects=True, vmem_limit_bytes=67043328 - 16 * chi_field.size - 16384
         ),
     )(chi_field, metric, curvature, trace_curvature, gamma_field, jnp.asarray(z_weights(), jnp.bfloat16))
+    count = float(chi_field.size * sizes[0] * sizes[1] * sizes[2])
+    return pl.pallas_call(
+        functools.partial(deliver, count),
+        out_shape=(
+            jax.ShapeDtypeStruct(chi_field.shape, jnp.float32),
+            jax.ShapeDtypeStruct(gamma_field.shape, jnp.float32),
+            jax.ShapeDtypeStruct((2,), jnp.float32),
+        ),
+        in_specs=[vmem, vmem, vmem],
+        out_specs=(hbm, hbm, hbm),
+        scratch_shapes=[pltpu.SMEM((2,), jnp.float32), pltpu.SemaphoreType.DMA((3,))],
+    )(*(pltpu.with_memory_space_constraint(v, pltpu.VMEM) for v in (ham, momentum, total)))
 
 
 def solution(mesh):

time: 43.7 us -> 39.2 us (0.90)
  local copies, waits for them, and re-layouts: 4.44 us -> 0 us
    unnamed x3 -> x0, local copies, waits for them, and re-layouts: 4.44 us -> none
    pallas_call x1 -> x2, Pallas kernels: 38.5 us -> 38.4 us  [the longest x1 37.6 us: on_device(): pl.pallas_call(functools.partial(kernel, sizes), out_shape=(pltpu.VMEM(ch...]
where the time goes in v1:
time: 39.2 us; the launch traced here: 39 us
  Pallas kernels  38.4 us (98%)
  between operations  0.64 us (2%)
    pallas_call x1, Pallas kernels, on_device(): pl.pallas_call(functools.partial(kernel, sizes), out_shape=(pltpu.VMEM(ch...  37.6 us
    pallas_call x1, Pallas kernels, on_device(): pl.pallas_call(functools.partial(deliver, count), out_shape=(jax.ShapeDty...  0.82 us

profile of v1, /device:TPU:0, one launch (start us, length us, event | category | flops | bytes accessed | tf_op | source)
XLA Modules:
  0.0 39.0 jit_solution(9705406962931118077)
XLA Ops:
  0.6 37.6 %shard_map.85 = (f32[8,32,128]{2,1,0:T(8,128)S(1)}, f32[3,8,32,128]{3,2,1,0:T(8,128)S(1)}, f32[8,128]{1,0:T(8,128)S(1)}) custom-call(f32[8,32,128]{2,1,0:T(8,128)} %chi_in.1, f32[6,8,32,128]{3,2,1,0:T(8,128)} %met_in.1, f32[6,8,32,128]{3,2,1,0:T(8,128)} %curv_in.1, f32[8,32,128]{2,1,0:T(8,128)} %trk_in.1, f32[3,8,32,128]{3,2,1,0:T(8,128)} %gam_in.1, ...), custom_call_target="tpu_custom_call" | custom-call | tf_op jit(solution)/shard_map/pallas_call | solution.py:454
  38.2 0.8 %shard_map.86 = (f32[8,32,128]{2,1,0:T(8,128)}, f32[3,8,32,128]{3,2,1,0:T(8,128)}, f32[2]{0:T(128)}) custom-call(f32[8,32,128]{2,1,0:T(8,128)S(1)} %get-tuple-element.6.ham_in, f32[3,8,32,128]{3,2,1,0:T(8,128)S(1)} %get-tuple-element.7.mom_in, f32[8,128]{1,0:T(8,128)S(1)} %get-tuple-element.8.total_in), custom_call_target="tpu_custom_call" | custom-call | tf_op jit(solution)/shard_map/pallas_call | solution.py:489

commit v2 on v1

--- a/solution.py
+++ b/solution.py
@@ -10,9 +10,9 @@
 
 pair_index = ((0, 1, 2), (1, 3, 4), (2, 4, 5))
 MESH = pl.DeviceIdType.MESH
-CHI, MET, CURV, TRK, GX, GY, GZ = 0, 1, 7, 13, 14, 15, 16
+GX, CHI, MET, CURV, TRK, GY, GZ = 0, 1, 2, 8, 14, 15, 16
 GEO = 7
-Z_FIELDS = tuple(range(14)) + (GZ,)
+Z_FIELDS = tuple(range(CHI, GY)) + (GZ,)
 TOP = 8
 
 
@@ -63,7 +63,7 @@
 
 
 def along_z(value, packed, weights):
-    parts = [jnp.concatenate([a, b], 1) for a, b in zip(split(value), split(packed))]
+    parts = [jnp.concatenate([a, b], 1) for a, b in zip(split(value), packed)]
     return sum(jnp.dot(part, weights, preferred_element_type=jnp.float32) for part in parts)
 
 
@@ -79,7 +79,7 @@
     return [m * scale for m in (m00, m01, m02, m11, m12, m22)]
 
 
-def cell_math(load, load_dx, load_dy, load_z, load_zz, load_xz, load_yz, load_part):
+def cell_math(load, load_dx, load_dy, load_z, load_zz, load_xz, load_yz):
     zpos = {f: n for n, f in enumerate(Z_FIELDS)}
     gu = inverse([load(MET + n, 0, 0) for n in range(6)])
     gu_hess = [12.0 * gu[n] if n in (0, 3, 5) else 2.0 * gu[n] for n in range(6)]
@@ -88,13 +88,14 @@
         c = load(f, 0, 0)
         xs = [load(f, s, 0) for s in (-2, -1, 1, 2)]
         ys = [load(f, 0, s) for s in (-2, -1, 1, 2)]
-        dx = load_dx(f, 0)
-        dy, dz = load_dy(f), load_z(f)
+        n = zpos[f]
+        dx = load_dx(n, 0)
+        dy, dz = load_dy(n), load_z(n)
         dxx = second(xs[0], xs[1], c, xs[2], xs[3])
         dyy = second(ys[0], ys[1], c, ys[2], ys[3])
-        dzz = load_zz(f)
-        dxy = first(*(load_dx(f, s) for s in (-2, -1, 1, 2)))
-        dxz, dyz = load_xz(f), load_yz(f)
+        dzz = load_zz(n)
+        dxy = first(*(load_dx(n, s) for s in (-2, -1, 1, 2)))
+        dxz, dyz = load_xz(n), load_yz(n)
         hess = (dxx, dxy, dxz, dyy, dyz, dzz)
         return (dx, dy, dz), total_of(gu_hess[n] * hess[n] for n in range(6))
 
@@ -172,7 +173,6 @@
     momentum = []
     for i in range(3):
         parts = total_of(sym(gu, j, k) * sym(curv_grads[j], k, i) for j in range(3) for k in range(3))
-        parts = parts + load_part(i)
         parts = parts - total_of(sym(curv, l, i) * push[l] for l in range(3))
         parts = parts - 0.5 * contract(curv_up, grads[i]) - (2.0 / 3.0) * trace_grads[i]
         momentum.append(parts * (1.0 / 12.0))
@@ -183,10 +183,10 @@
     sizes,
     chi_in, met_in, curv_in, trk_in, gam_in, weights_in,
     ham_out, mom_out, total_out,
-    cells, packed, pack_own, pack_left, pack_right, slope, sums,
-    part_out, part, weights, z_one, z_two, y_one, yz_two, xz_two,
+    cells, packed, pack_own, pack_left, pack_right, edge_own, edge_left, edge_right, slope, sums,
+    part_out, part, weights, z_one, z_two, y_one, yz_two, xz_two, mid_split, dy_split, dx_split,
     slots_x, slots_y,
-    load_sem, xs, xr, ys, yr, zs, zr, es, er, pxs, pxr, pys, pyr,
+    load_sem, xs, xr, ys, yr, zs, zr, es, er, pys, pyr, ezs, ezr,
     rxs, rxr, rys, ryr, cs, cr,
 ):
     nx, ny, nz = sizes
@@ -219,11 +219,12 @@
         pltpu.make_async_copy(src, dst, load_sem.at[n])
         for n, (src, dst) in enumerate(
             (
+                (met_in, cells.at[pl.ds(MET, 6), own_x, own_y]),
                 (chi_in, cells.at[CHI, own_x, own_y]),
-                (met_in, cells.at[pl.ds(MET, 6), own_x, own_y]),
+                (gam_in.at[0], cells.at[GX, own_x, own_y]),
                 (curv_in, cells.at[pl.ds(CURV, 6), own_x, own_y]),
                 (trk_in, cells.at[TRK, own_x, own_y]),
-                (gam_in, cells.at[pl.ds(GX, 3), own_x, own_y]),
+                (gam_in.at[pl.ds(1, 2)], cells.at[pl.ds(GY, 2), own_x, own_y]),
                 (weights_in, weights),
             )
         )
@@ -244,97 +245,175 @@
         copy.start()
         return copy
 
-    for copy in loads[:5]:
-        copy.wait()
     low_x, high_x = pl.ds(2, 2), pl.ds(cx, 2)
-    x_faces = []
-    for n, fields in enumerate((pl.ds(0, GEO), pl.ds(GX, 1))):
-        x_faces += [
-            send(cells.at[fields, high_x, own_y], cells.at[fields, pl.ds(0, 2), own_y], xs.at[2 * n], xr.at[2 * n], 0, 1),
-            send(cells.at[fields, low_x, own_y], cells.at[fields, pl.ds(cx + 2, 2), own_y], xs.at[2 * n + 1], xr.at[2 * n + 1], 0, -1),
-        ]
+    before_x, after_x = pl.ds(0, 2), pl.ds(cx + 2, 2)
     low_y, high_y = pl.ds(TOP, 2), pl.ds(TOP + cy - 2, 2)
     before_y, after_y = pl.ds(TOP - 2, 2), pl.ds(TOP + cy, 2)
-    y_faces = [
-        send(cells.at[pl.ds(0, 16), own_x, high_y], cells.at[pl.ds(0, 16), own_x, before_y], ys.at[0], yr.at[0], 1, 1),
-        send(cells.at[pl.ds(0, 16), own_x, low_y], cells.at[pl.ds(0, 16), own_x, after_y], ys.at[1], yr.at[1], 1, -1),
-    ]
+    x_faces, y_faces = [], []
+
+    def send_x(fields):
+        n = len(x_faces)
+        x_faces.extend((
+            send(cells.at[fields, high_x, own_y], cells.at[fields, before_x, own_y], xs.at[n], xr.at[n], 0, 1),
+            send(cells.at[fields, low_x, own_y], cells.at[fields, after_x, own_y], xs.at[n + 1], xr.at[n + 1], 0, -1),
+        ))
+
+    def send_y(fields):
+        n = len(y_faces)
+        y_faces.extend((
+            send(cells.at[fields, own_x, high_y], cells.at[fields, own_x, before_y], ys.at[n], yr.at[n], 1, 1),
+            send(cells.at[fields, own_x, low_y], cells.at[fields, own_x, after_y], ys.at[n + 1], yr.at[n + 1], 1, -1),
+        ))
+
+    loads[0].wait()
+    send_x(pl.ds(MET, 6))
+    loads[1].wait()
+    send_x(pl.ds(CHI, 1))
+    send_y(pl.ds(CHI, GEO))
+    loads[2].wait()
+    send_x(pl.ds(GX, 1))
+    for copy in loads[3:6]:
+        copy.wait()
+    send_y(pl.ds(CURV, 8))
+
     tiles = cy // 8
-    lane = lax.broadcasted_iota(jnp.int32, (8, 128), 1)
-
-    def pack(step, carry):
-        x, y = step // tiles, lax.rem(step, tiles) * 8
-        rows = pl.ds(pl.multiple_of(TOP + y, 8), 8)
-        value = jnp.zeros((8, 128), jnp.float32)
-        group = lax.shift_right_logical(lane, 2)
-        for n, f in enumerate(Z_FIELDS):
-            value = jnp.where(group == n, pltpu.roll(cells[f, x + 2, rows], 4 * n + 2, 1), value)
-        pack_own[x, pl.ds(pl.multiple_of(y, 8), 8)] = value
-        return carry
-
-    lax.fori_loop(0, cx * tiles, pack, 0)
+    group = lax.shift_right_logical(lax.broadcasted_iota(jnp.int32, (8, 128), 1), 2)
+    far_side = (lax.broadcasted_iota(jnp.int32, (cy, 128), 1) & 2) != 0
+
+    def packing(fields, target, layer):
+        def pack(step, carry):
+            at, y = step // tiles, lax.rem(step, tiles) * 8
+            rows = pl.ds(pl.multiple_of(TOP + y, 8), 8)
+            x = layer(at)
+            picked = [
+                jnp.where(group == n, pltpu.roll(cells[f, x, rows], 4 * n + 2, 1), 0.0)
+                for n, f in enumerate(fields)
+            ]
+            target[at, pl.ds(pl.multiple_of(y, 8), 8)] = total_of(picked)
+            return carry
+
+        lax.fori_loop(0, target.shape[0] * tiles, pack, 0, unroll=4)
+
+    packing(Z_FIELDS, pack_own, lambda at: at + 2)
     z_faces = [
         send(pack_own, pack_left, zs.at[0], zr.at[0], 2, 1),
         send(pack_own, pack_right, zs.at[1], zr.at[1], 2, -1),
     ]
+    sums[...] = jnp.zeros_like(sums)
+    missing = jnp.zeros((7, 2, cy, 128), jnp.float32)
+    cells[pl.ds(CURV, 7), before_x, own_y] = missing
+    cells[pl.ds(CURV, 7), after_x, own_y] = missing
     for copy in z_faces:
         copy.wait_recv()
 
+    def keep_split(target, value, at=0):
+        for n, half in enumerate(split(value)):
+            target[n, pl.ds(at, value.shape[0])] = half
+
     def merge(x, carry):
-        wide = lax.broadcasted_iota(jnp.int32, (cy, 128), 1)
-        packed[x + 2, own_y] = jnp.where((wide & 2) == 0, pack_left[x], pack_right[x])
+        value = jnp.where(far_side, pack_right[x], pack_left[x])
+        packed[x + 2, own_y] = value
+        keep_split(mid_split, value, pl.multiple_of(x * cy, cy))
         return carry
 
     lax.fori_loop(0, cx, merge, 0)
-    px_faces = [
-        send(packed.at[high_x, own_y], packed.at[pl.ds(0, 2), own_y], pxs.at[0], pxr.at[0], 0, 1),
-        send(packed.at[low_x, own_y], packed.at[pl.ds(cx + 2, 2), own_y], pxs.at[1], pxr.at[1], 0, -1),
-    ]
     py_faces = [
         send(packed.at[own_x, high_y], packed.at[own_x, before_y], pys.at[0], pyr.at[0], 1, 1),
         send(packed.at[own_x, low_y], packed.at[own_x, after_y], pys.at[1], pyr.at[1], 1, -1),
     ]
-    edges = []
-    for n, rows in enumerate((before_y, after_y)):
-        y_faces[n].wait_recv()
-        edges += [
-            send(cells.at[pl.ds(0, GEO), high_x, rows], cells.at[pl.ds(0, GEO), pl.ds(0, 2), rows], es.at[2 * n], er.at[2 * n], 0, 1),
-            send(cells.at[pl.ds(0, GEO), low_x, rows], cells.at[pl.ds(0, GEO), pl.ds(cx + 2, 2), rows], es.at[2 * n + 1], er.at[2 * n + 1], 0, -1),
-        ]
-    for copy in py_faces:
-        copy.wait_recv()
-
-    sums[...] = jnp.zeros_like(sums)
-    loads[5].wait()
+    loads[6].wait()
     flat = (cx * cy, 128)
 
-    def geo_z(f, carry):
-        mid = packed[own_x, own_y].reshape(flat)
-        both = along_z(cells[f, own_x, own_y].reshape(flat), mid, weights[f])
-        z_one[f] = both[:, :128].reshape(cx, cy, 128)
-        z_two[f] = both[:, 128:].reshape(cx, cy, 128)
-        dy = first(*(cells[f, own_x, pl.ds(TOP + s, cy)] for s in (-2, -1, 1, 2)))
-        dy_packed = first(*(packed[own_x, pl.ds(TOP + s, cy)] for s in (-2, -1, 1, 2)))
-        y_one[f] = dy
-        yz_two[f] = along_z(dy.reshape(flat), dy_packed.reshape(flat), weights[f, :, :128]).reshape(cx, cy, 128)
-        return carry
-
-    lax.fori_loop(0, GEO, geo_z, 0)
+    def geo_z(n, carry):
+        both = along_z(cells[n + CHI, own_x, own_y].reshape(flat), mid_split[...], weights[n])
+        z_one[n] = both[:, :128].reshape(cx, cy, 128)
+        z_two[n] = both[:, 128:].reshape(cx, cy, 128)
+        return carry
+
+    lax.fori_loop(0, GEO, geo_z, 0, unroll=7)
 
     def rest_z(n, carry):
-        f = jnp.where(n == 14, GZ, n)
-        mid = packed[own_x, own_y].reshape(flat)
-        z_one[n] = along_z(cells[f, own_x, own_y].reshape(flat), mid, weights[n, :, :128]).reshape(cx, cy, 128)
-        return carry
-
-    lax.fori_loop(GEO, len(Z_FIELDS), rest_z, 0)
-
-    part[:, pl.ds(2, cx - 4)] = jnp.zeros((3, cx - 4, cy, 128), jnp.float32)
-    missing = jnp.zeros((7, 2, cy, 128), jnp.float32)
-    cells[pl.ds(CURV, 7), pl.ds(0, 2), own_y] = missing
-    cells[pl.ds(CURV, 7), pl.ds(cx + 2, 2), own_y] = missing
-    x_faces[0].wait_recv()
-    x_faces[1].wait_recv()
+        f = n + CHI + n // (GY - CHI)
+        z_one[n] = along_z(
+            cells[f, own_x, own_y].reshape(flat), mid_split[...], weights[n, :, :128]
+        ).reshape(cx, cy, 128)
+        return carry
+
+    lax.fori_loop(GEO, len(Z_FIELDS), rest_z, 0, unroll=8)
+
+    for copy in y_faces[:2] + py_faces:
+        copy.wait_recv()
+    keep_split(dy_split, first(*(packed[own_x, pl.ds(TOP + s, cy)] for s in (-2, -1, 1, 2))).reshape(flat))
+
+    def geo_y(n, carry):
+        dy = first(*(cells[n + CHI, own_x, pl.ds(TOP + s, cy)] for s in (-2, -1, 1, 2)))
+        y_one[n] = dy
+        yz_two[n] = along_z(dy.reshape(flat), dy_split[...], weights[n, :, :128]).reshape(cx, cy, 128)
+        return carry
+
+    lax.fori_loop(0, GEO, geo_y, 0, unroll=7)
+
+    def slopes(pieces):
+        rows = [count * cy for _, count in pieces]
+        at = 0
+        for (base, count), size in zip(pieces, rows):
+            values = first(*(packed[pl.ds(base + 2 + s, count), own_y] for s in (-2, -1, 1, 2)))
+            keep_split(dx_split, values.reshape(size, 128), at)
+            at += size
+        total = at
+
+        def one(n, carry):
+            values = []
+            for (base, count), size in zip(pieces, rows):
+                dx = first(*(cells[n + CHI, pl.ds(base + 2 + s, count), pl.ds(TOP - 8, cy + 16)] for s in (-2, -1, 1, 2)))
+                slope[n, pl.ds(base, count)] = dx
+                values.append(dx[:, TOP : TOP + cy].reshape(size, 128))
+            both = along_z(jnp.concatenate(values, 0), dx_split[:, :total], weights[n, :, :128])
+            at = 0
+            for (base, count), size in zip(pieces, rows):
+                xz_two[n, pl.ds(base, count)] = both[at : at + size].reshape(count, cy, 128)
+                at += size
+            return carry
+
+        lax.fori_loop(0, GEO, one, 0, unroll=7)
+
+    def tile_at(x, y):
+        rows = pl.ds(pl.multiple_of(y, 8), 8)
+        ham, momentum = cell_math(
+            lambda f, sx, sy: cells[f, x + 2 + sx, pl.ds(TOP + y + sy, 8)],
+            lambda n, sy: slope[n, x, pl.ds(TOP + y + sy, 8)],
+            lambda n: y_one[n, x, rows],
+            lambda n: z_one[n, x, rows],
+            lambda n: z_two[n, x, rows],
+            lambda n: xz_two[n, x, rows],
+            lambda n: yz_two[n, x, rows],
+        )
+        ham_out[x, rows] = ham
+        for i in range(3):
+            mom_out[i, x, rows] = momentum[i]
+        sums[0] += ham * ham
+        return momentum
+
+    def inner(n, carry):
+        momentum = tile_at(2 + n // tiles, lax.rem(n, tiles) * 8)
+        sums[1] += momentum[0] * momentum[0] + momentum[1] * momentum[1] + momentum[2] * momentum[2]
+        return carry
+
+    def outer(n, carry):
+        tile_at(outer_x(n // tiles), lax.rem(n, tiles) * 8)
+        return carry
+
+    def outer_x(at):
+        return at + at // 2 * (cx - 4)
+
+    slopes(((2, cx - 4),))
+    for copy in y_faces[2:]:
+        copy.wait_recv()
+    inner_tiles = (cx - 4) * tiles
+    cut = inner_tiles * 8 // 16, inner_tiles * 12 // 16
+    lax.fori_loop(0, cut[0], inner, 0)
+    for copy in x_faces[:2]:
+        copy.wait_recv()
 
     def offer(t, carry):
         rows = pl.ds(pl.multiple_of(TOP + t * 8, 8), 8)
@@ -351,57 +430,54 @@
                     value = total_of(sym(gu, 0, k) * sym(values, k, i) for k in range(3))
                     if i == 0:
                         value = value - (2.0 / 3.0) * values[6]
-                    part_out[side, i, slot, out_rows] = value
+                    part_out[side, i, slot, out_rows] = value * (1.0 / 12.0)
         return carry
 
     lax.fori_loop(0, tiles, offer, 0)
     part_faces = [
-        send(part_out.at[0], part.at[:, pl.ds(cx - 2, 2)], cs.at[0], cr.at[0], 0, -1),
+        send(part_out.at[0], part.at[:, pl.ds(2, 2)], cs.at[0], cr.at[0], 0, -1),
         send(part_out.at[1], part.at[:, pl.ds(0, 2)], cs.at[1], cr.at[1], 0, 1),
     ]
-
-    def group(step, carry):
-        base = lax.rem(2 * step + 2, cx)
-
-        @pl.when(2 * step == cx - 4)
-        def _():
-            for copy in x_faces[2:] + px_faces + edges + part_faces:
-                copy.wait_recv()
-
-        def slopes(f, inner):
-            slope[f] = first(*(cells[f, pl.ds(base + 2 + s, 2)] for s in (-2, -1, 1, 2)))
-            dx = slope[f, :, own_y].reshape(2 * cy, 128)
-            dx_packed = first(*(packed[pl.ds(base + 2 + s, 2), own_y] for s in (-2, -1, 1, 2)))
-            xz_two[f] = along_z(dx, dx_packed.reshape(2 * cy, 128), weights[f, :, :128]).reshape(2, cy, 128)
-            return inner
-
-        lax.fori_loop(0, GEO, slopes, 0)
-
-        def tile(n, inner):
-            half, y = n // tiles, lax.rem(n, tiles) * 8
-            x = base + half
-            rows = pl.ds(pl.multiple_of(y, 8), 8)
-            ham, momentum = cell_math(
-                lambda f, sx, sy: cells[f, x + 2 + sx, pl.ds(TOP + y + sy, 8)],
-                lambda f, sy: slope[f, half, pl.ds(TOP + y + sy, 8)],
-                lambda f: y_one[f, x, rows],
-                lambda f: z_one[f, x, rows],
-                lambda f: z_two[f, x, rows],
-                lambda f: xz_two[f, half, rows],
-                lambda f: yz_two[f, x, rows],
-                lambda i: part[i, x, rows],
-            )
-            ham_out[x, rows] = ham
-            for i in range(3):
-                mom_out[i, x, rows] = momentum[i]
-            sums[0] += ham * ham
-            sums[1] += momentum[0] * momentum[0] + momentum[1] * momentum[1] + momentum[2] * momentum[2]
-            return inner
-
-        lax.fori_loop(0, 2 * tiles, tile, 0)
-        return carry
-
-    lax.fori_loop(0, cx // 2, group, 0)
+    lax.fori_loop(cut[0], cut[1], inner, 0)
+    for copy in x_faces[2:4]:
+        copy.wait_recv()
+    geo = pl.ds(CHI, GEO)
+    edges = []
+    for layers in (before_x, after_x):
+        n = len(edges)
+        edges += [
+            send(cells.at[geo, layers, high_y], cells.at[geo, layers, before_y], es.at[n], er.at[n], 1, 1),
+            send(cells.at[geo, layers, low_y], cells.at[geo, layers, after_y], es.at[n + 1], er.at[n + 1], 1, -1),
+        ]
+    packing(Z_FIELDS[:GEO], edge_own, lambda at: at + at // 2 * cx)
+    edge_z = [
+        send(edge_own, edge_left, ezs.at[0], ezr.at[0], 2, 1),
+        send(edge_own, edge_right, ezs.at[1], ezr.at[1], 2, -1),
+    ]
+    lax.fori_loop(cut[1], inner_tiles, inner, 0)
+    for copy in edge_z:
+        copy.wait_recv()
+    for at in range(4):
+        packed[at + at // 2 * cx, own_y] = jnp.where(far_side, edge_right[at], edge_left[at])
+    for copy in edges:
+        copy.wait_recv()
+    slopes(((0, 2), (cx - 2, 2)))
+    for copy in x_faces[4:]:
+        copy.wait_recv()
+    lax.fori_loop(0, 4 * tiles, outer, 0)
+    for copy in part_faces:
+        copy.wait_recv()
+
+    def finish(n, carry):
+        at, rows = n // tiles, pl.ds(pl.multiple_of(lax.rem(n, tiles) * 8, 8), 8)
+        x = outer_x(at)
+        momentum = [mom_out[i, x, rows] + part[i, at, rows] for i in range(3)]
+        for i in range(3):
+            mom_out[i, x, rows] = momentum[i]
+        sums[1] += momentum[0] * momentum[0] + momentum[1] * momentum[1] + momentum[2] * momentum[2]
+        return carry
+
+    lax.fori_loop(0, 4 * tiles, finish, 0, unroll=4)
 
     row = lax.broadcasted_iota(jnp.int32, (8, 128), 0)
     ham_sum = jnp.sum(sums[0], axis=0, keepdims=True)
@@ -422,7 +498,7 @@
             ).wait_recv()
         total = total_of(slots[n] for n in range(len(others) + 1))
     total_out[...] = total
-    for copy in x_faces + y_faces + z_faces + px_faces + py_faces + edges + part_faces + pending:
+    for copy in x_faces + y_faces + z_faces + py_faces + edges + edge_z + part_faces + pending:
         copy.wait_send()
 
 
@@ -463,23 +539,21 @@
         scratch_shapes=[
             pltpu.VMEM((17,) + block, jnp.float32),
             pltpu.VMEM(block, jnp.float32),
-            pltpu.VMEM((cx, cy, cz), jnp.float32),
-            pltpu.VMEM((cx, cy, cz), jnp.float32),
-            pltpu.VMEM((cx, cy, cz), jnp.float32),
-            pltpu.VMEM((GEO, 2) + block[1:], jnp.float32),
+        ]
+        + [pltpu.VMEM((cx, cy, cz), jnp.float32)] * 3
+        + [pltpu.VMEM((4, cy, cz), jnp.float32)] * 3
+        + [
+            pltpu.VMEM((GEO, cx) + block[1:], jnp.float32),
             pltpu.VMEM((2, 8, 128), jnp.float32),
             pltpu.VMEM((2, 3, 2, cy, cz), jnp.float32),
-            pltpu.VMEM((3, cx, cy, cz), jnp.float32),
+            pltpu.VMEM((3, 4, cy, cz), jnp.float32),
             pltpu.VMEM((len(Z_FIELDS), 256, 256), jnp.bfloat16),
             pltpu.VMEM((len(Z_FIELDS), cx, cy, cz), jnp.float32),
-            pltpu.VMEM((GEO, cx, cy, cz), jnp.float32),
-            pltpu.VMEM((GEO, cx, cy, cz), jnp.float32),
-            pltpu.VMEM((GEO, cx, cy, cz), jnp.float32),
-            pltpu.VMEM((GEO, 2, cy, cz), jnp.float32),
         ]
+        + [pltpu.VMEM((GEO, cx, cy, cz), jnp.float32)] * 4
+        + [pltpu.VMEM((2, cx * cy, cz), jnp.bfloat16)] * 3
         + [pltpu.VMEM((n, 8, 128), jnp.float32) for n in (sizes[0], sizes[1] * sizes[2])]
-        + [dma((6,)), dma((4,)), dma((4,)), dma((2,)), dma((2,)), dma((2,)), dma((2,))]
-        + [dma((4,)), dma((4,)), dma((2,)), dma((2,)), dma((2,)), dma((2,))]
+        + [dma((n,)) for n in (7, 6, 6, 4, 4, 2, 2, 4, 4, 2, 2, 2, 2)]
         + [dma((n,)) for n in (sizes[0], sizes[1] * sizes[2], 2) for _ in range(2)],
         compiler_params=pltpu.CompilerParams(
             collective_id=0, has_side_effects=True, vmem_limit_bytes=67043328 - 16 * chi_field.size - 16384

time: 39.2 us -> 34.4 us (0.88)
  Pallas kernels: 38.4 us -> 33.6 us
    pallas_call x1, Pallas kernels: 37.6 us -> 32.8 us  [on_device(): pl.pallas_call(functools.partial(kernel, sizes), out_shape=(pltpu.VMEM(ch...]
where the time goes in v2:
time: 34.4 us; the launch traced here: 34.3 us
  Pallas kernels  33.6 us (98%)
  between operations  0.64 us (2%)
    pallas_call x1, Pallas kernels, on_device(): pl.pallas_call(functools.partial(kernel, sizes), out_shape=(pltpu.VMEM(ch...  32.8 us
    pallas_call x1, Pallas kernels, on_device(): pl.pallas_call(functools.partial(deliver, count), out_shape=(jax.ShapeDty...  0.82 us

profile of v2, /device:TPU:0, one launch (start us, length us, event | category | flops | bytes accessed | tf_op | source)
XLA Modules:
  0.0 34.3 jit_solution(1908687064328981485)
XLA Ops:
  0.6 32.8 %shard_map.85 = (f32[8,32,128]{2,1,0:T(8,128)S(1)}, f32[3,8,32,128]{3,2,1,0:T(8,128)S(1)}, f32[8,128]{1,0:T(8,128)S(1)}) custom-call(f32[8,32,128]{2,1,0:T(8,128)} %chi_in.1, f32[6,8,32,128]{3,2,1,0:T(8,128)} %met_in.1, f32[6,8,32,128]{3,2,1,0:T(8,128)} %curv_in.1, f32[8,32,128]{2,1,0:T(8,128)} %trk_in.1, f32[3,8,32,128]{3,2,1,0:T(8,128)} %gam_in.1, ...), custom_call_target="tpu_custom_call" | custom-call | tf_op jit(solution)/shard_map/pallas_call | solution.py:530
  33.5 0.8 %shard_map.86 = (f32[8,32,128]{2,1,0:T(8,128)}, f32[3,8,32,128]{3,2,1,0:T(8,128)}, f32[2]{0:T(128)}) custom-call(f32[8,32,128]{2,1,0:T(8,128)S(1)} %get-tuple-element.6.ham_in, f32[3,8,32,128]{3,2,1,0:T(8,128)S(1)} %get-tuple-element.7.mom_in, f32[8,128]{1,0:T(8,128)S(1)} %get-tuple-element.8.total_in), custom_call_target="tpu_custom_call" | custom-call | tf_op jit(solution)/shard_map/pallas_call | solution.py:563

commit v3 on v2

--- a/solution.py
+++ b/solution.py
@@ -229,7 +229,7 @@
             )
         )
     ]
-    for copy in loads:
+    for copy in loads[:6]:
         copy.start()
     barrier = pltpu.get_barrier_semaphore()
     for axes in ((1, 2), (0,)):
@@ -275,6 +275,7 @@
     for copy in loads[3:6]:
         copy.wait()
     send_y(pl.ds(CURV, 8))
+    loads[6].start()
 
     tiles = cy // 8
     group = lax.shift_right_logical(lax.broadcasted_iota(jnp.int32, (8, 128), 1), 2)
@@ -288,6 +289,7 @@
             picked = [
                 jnp.where(group == n, pltpu.roll(cells[f, x, rows], 4 * n + 2, 1), 0.0)
                 for n, f in enumerate(fields)
+                if f is not None
             ]
             target[at, pl.ds(pl.multiple_of(y, 8), 8)] = total_of(picked)
             return carry
@@ -295,10 +297,17 @@
         lax.fori_loop(0, target.shape[0] * tiles, pack, 0, unroll=4)
 
     packing(Z_FIELDS, pack_own, lambda at: at + 2)
-    z_faces = [
-        send(pack_own, pack_left, zs.at[0], zr.at[0], 2, 1),
-        send(pack_own, pack_right, zs.at[1], zr.at[1], 2, -1),
-    ]
+
+    def send_z(own, left, right, send_sem, recv_sem):
+        faces = [send(own, left, send_sem.at[0], recv_sem.at[0], 2, 1)]
+        if nz > 2:
+            faces.append(send(own, right, send_sem.at[1], recv_sem.at[1], 2, -1))
+        return faces
+
+    def joined(left, right, at):
+        return jnp.where(far_side, right[at], left[at]) if nz > 2 else left[at]
+
+    z_faces = send_z(pack_own, pack_left, pack_right, zs, zr)
     sums[...] = jnp.zeros_like(sums)
     missing = jnp.zeros((7, 2, cy, 128), jnp.float32)
     cells[pl.ds(CURV, 7), before_x, own_y] = missing
@@ -311,7 +320,7 @@
             target[n, pl.ds(at, value.shape[0])] = half
 
     def merge(x, carry):
-        value = jnp.where(far_side, pack_right[x], pack_left[x])
+        value = joined(pack_left, pack_right, x)
         packed[x + 2, own_y] = value
         keep_split(mid_split, value, pl.multiple_of(x * cy, cy))
         return carry
@@ -341,17 +350,29 @@
 
     lax.fori_loop(GEO, len(Z_FIELDS), rest_z, 0, unroll=8)
 
-    for copy in y_faces[:2] + py_faces:
-        copy.wait_recv()
-    keep_split(dy_split, first(*(packed[own_x, pl.ds(TOP + s, cy)] for s in (-2, -1, 1, 2))).reshape(flat))
-
-    def geo_y(n, carry):
-        dy = first(*(cells[n + CHI, own_x, pl.ds(TOP + s, cy)] for s in (-2, -1, 1, 2)))
-        y_one[n] = dy
-        yz_two[n] = along_z(dy.reshape(flat), dy_split[...], weights[n, :, :128]).reshape(cx, cy, 128)
-        return carry
-
-    lax.fori_loop(0, GEO, geo_y, 0, unroll=7)
+    def rises(pieces):
+        rows = [cx * count for _, count in pieces]
+        at = 0
+        for (row, count), size in zip(pieces, rows):
+            values = first(*(packed[own_x, pl.ds(TOP + row + s, count)] for s in (-2, -1, 1, 2)))
+            keep_split(dy_split, values.reshape(size, 128), at)
+            at += size
+        total = at
+
+        def one(n, carry):
+            values = []
+            for (row, count), size in zip(pieces, rows):
+                dy = first(*(cells[n + CHI, own_x, pl.ds(TOP + row + s, count)] for s in (-2, -1, 1, 2)))
+                y_one[n, :, pl.ds(row, count)] = dy
+                values.append(dy.reshape(size, 128))
+            both = along_z(jnp.concatenate(values, 0), dy_split[:, :total], weights[n, :, :128])
+            at = 0
+            for (row, count), size in zip(pieces, rows):
+                yz_two[n, :, pl.ds(row, count)] = both[at : at + size].reshape(cx, count, 128)
+                at += size
+            return carry
+
+        lax.fori_loop(0, GEO, one, 0, unroll=7)
 
     def slopes(pieces):
         rows = [count * cy for _, count in pieces]
@@ -365,9 +386,9 @@
         def one(n, carry):
             values = []
             for (base, count), size in zip(pieces, rows):
-                dx = first(*(cells[n + CHI, pl.ds(base + 2 + s, count), pl.ds(TOP - 8, cy + 16)] for s in (-2, -1, 1, 2)))
-                slope[n, pl.ds(base, count)] = dx
-                values.append(dx[:, TOP : TOP + cy].reshape(size, 128))
+                dx = first(*(cells[n + CHI, pl.ds(base + 2 + s, count), own_y] for s in (-2, -1, 1, 2)))
+                slope[n, pl.ds(base, count), own_y] = dx
+                values.append(dx.reshape(size, 128))
             both = along_z(jnp.concatenate(values, 0), dx_split[:, :total], weights[n, :, :128])
             at = 0
             for (base, count), size in zip(pieces, rows):
@@ -394,24 +415,43 @@
         sums[0] += ham * ham
         return momentum
 
-    def inner(n, carry):
-        momentum = tile_at(2 + n // tiles, lax.rem(n, tiles) * 8)
-        sums[1] += momentum[0] * momentum[0] + momentum[1] * momentum[1] + momentum[2] * momentum[2]
-        return carry
-
-    def outer(n, carry):
-        tile_at(outer_x(n // tiles), lax.rem(n, tiles) * 8)
-        return carry
+    def rims(pieces):
+        def one(n, carry):
+            for base, count in pieces:
+                for rows in (pl.ds(TOP - 8, 8), pl.ds(TOP + cy, 8)):
+                    slope[n, pl.ds(base, count), rows] = first(
+                        *(cells[n + CHI, pl.ds(base + 2 + s, count), rows] for s in (-2, -1, 1, 2))
+                    )
+            return carry
+
+        lax.fori_loop(0, GEO, one, 0, unroll=7)
 
     def outer_x(at):
         return at + at // 2 * (cx - 4)
 
+    def run(layers, layer, count, row, square):
+        def one(n, carry):
+            momentum = tile_at(layer(n // count), row(lax.rem(n, count)))
+            if square:
+                sums[1] += momentum[0] * momentum[0] + momentum[1] * momentum[1] + momentum[2] * momentum[2]
+            return carry
+
+        lax.fori_loop(0, layers * count, one, 0)
+
+    inner = (cx - 4, lambda at: at + 2)
+    outer = (4, outer_x)
+    middle = (tiles - 2, lambda at: 8 * at + 8)
+    rim = (2, lambda at: at * (cy - 8))
+    rises(((8, cy - 16),))
     slopes(((2, cx - 4),))
+    run(*inner, *middle, True)
+    for copy in y_faces[:2] + py_faces:
+        copy.wait_recv()
+    rises(((0, 8), (cy - 8, 8)))
+    rims(((2, cx - 4),))
     for copy in y_faces[2:]:
         copy.wait_recv()
-    inner_tiles = (cx - 4) * tiles
-    cut = inner_tiles * 8 // 16, inner_tiles * 12 // 16
-    lax.fori_loop(0, cut[0], inner, 0)
+    run(*inner, *rim, True)
     for copy in x_faces[:2]:
         copy.wait_recv()
 
@@ -438,33 +478,39 @@
         send(part_out.at[0], part.at[:, pl.ds(2, 2)], cs.at[0], cr.at[0], 0, -1),
         send(part_out.at[1], part.at[:, pl.ds(0, 2)], cs.at[1], cr.at[1], 0, 1),
     ]
-    lax.fori_loop(cut[0], cut[1], inner, 0)
+    edges, edge_z = [], []
+
+    def relay(fields):
+        for layers in (before_x, after_x):
+            n = len(edges)
+            edges.extend((
+                send(cells.at[fields, layers, high_y], cells.at[fields, layers, before_y], es.at[n], er.at[n], 1, 1),
+                send(cells.at[fields, layers, low_y], cells.at[fields, layers, after_y], es.at[n + 1], er.at[n + 1], 1, -1),
+            ))
+
+    def relay_z(fields):
+        n = len(edge_z)
+        packing(fields, edge_own.at[n], lambda at: at + at // 2 * cx)
+        edge_z.append(send_z(edge_own.at[n], edge_left.at[n], edge_right.at[n], ezs.at[n], ezr.at[n]))
+
+    relay(pl.ds(MET, 6))
+    relay_z((None,) + tuple(range(MET, CURV)))
     for copy in x_faces[2:4]:
         copy.wait_recv()
-    geo = pl.ds(CHI, GEO)
-    edges = []
-    for layers in (before_x, after_x):
-        n = len(edges)
-        edges += [
-            send(cells.at[geo, layers, high_y], cells.at[geo, layers, before_y], es.at[n], er.at[n], 1, 1),
-            send(cells.at[geo, layers, low_y], cells.at[geo, layers, after_y], es.at[n + 1], er.at[n + 1], 1, -1),
-        ]
-    packing(Z_FIELDS[:GEO], edge_own, lambda at: at + at // 2 * cx)
-    edge_z = [
-        send(edge_own, edge_left, ezs.at[0], ezr.at[0], 2, 1),
-        send(edge_own, edge_right, ezs.at[1], ezr.at[1], 2, -1),
-    ]
-    lax.fori_loop(cut[1], inner_tiles, inner, 0)
-    for copy in edge_z:
+    relay(pl.ds(CHI, 1))
+    relay_z((CHI,))
+    for copy in edge_z[0] + edge_z[1]:
         copy.wait_recv()
     for at in range(4):
-        packed[at + at // 2 * cx, own_y] = jnp.where(far_side, edge_right[at], edge_left[at])
-    for copy in edges:
-        copy.wait_recv()
+        packed[at + at // 2 * cx, own_y] = joined(edge_left.at[0], edge_right.at[0], at) + joined(edge_left.at[1], edge_right.at[1], at)
     slopes(((0, 2), (cx - 2, 2)))
     for copy in x_faces[4:]:
         copy.wait_recv()
-    lax.fori_loop(0, 4 * tiles, outer, 0)
+    run(*outer, *middle, False)
+    for copy in edges:
+        copy.wait_recv()
+    rims(((0, 2), (cx - 2, 2)))
+    run(*outer, *rim, False)
     for copy in part_faces:
         copy.wait_recv()
 
@@ -479,26 +525,26 @@
 
     lax.fori_loop(0, 4 * tiles, finish, 0, unroll=4)
 
-    row = lax.broadcasted_iota(jnp.int32, (8, 128), 0)
-    ham_sum = jnp.sum(sums[0], axis=0, keepdims=True)
-    mom_sum = jnp.sum(sums[1], axis=0, keepdims=True)
-    total = jnp.where(row == 0, ham_sum, jnp.where(row == 1, mom_sum, 0.0))
+    lane = lax.broadcasted_iota(jnp.int32, (8, 128), 1)
+    folded = [sums[n] + pltpu.roll(sums[n], 64, 1) for n in range(2)]
+    total = jnp.sum(jnp.where(lane < 64, folded[0], folded[1]), axis=0, keepdims=True)
+    line = pl.ds(0, 1)
     pending = []
     for axes, slots, ss, rs in (((1, 2), slots_y, rys, ryr), ((0,), slots_x, rxs, rxr)):
         here = place_in(axes)
-        slots[here] = total
+        slots[here, line] = total
         others = hops(axes)
         for n, step in enumerate(others):
-            pending.append(send(slots.at[here], slots.at[here], ss.at[n], rs.at[here], axes, step))
+            pending.append(send(slots.at[here, line], slots.at[here, line], ss.at[n], rs.at[here], axes, step))
         for n, step in enumerate(others):
             source = place_in(axes, step)
             pltpu.make_async_remote_copy(
-                src_ref=slots.at[source], dst_ref=slots.at[source], send_sem=ss.at[n],
+                src_ref=slots.at[source, line], dst_ref=slots.at[source, line], send_sem=ss.at[n],
                 recv_sem=rs.at[source], device_id=peer(axes, step), device_id_type=MESH,
             ).wait_recv()
-        total = total_of(slots[n] for n in range(len(others) + 1))
+        total = total_of(slots[n, line] for n in range(len(others) + 1))
     total_out[...] = total
-    for copy in x_faces + y_faces + z_faces + py_faces + edges + edge_z + part_faces + pending:
+    for copy in x_faces + y_faces + z_faces + py_faces + edges + edge_z[0] + edge_z[1] + part_faces + pending:
         copy.wait_send()
 
 
@@ -509,11 +555,11 @@
     ]
     for copy in copies:
         copy.start()
-    row = lax.broadcasted_iota(jnp.int32, (8, 128), 0)
-    rates = jnp.where(row == 0, 1.0 / count, 1.0 / (3.0 * count))
-    root = jnp.sqrt(jnp.sum(total_in[...] * rates, axis=1, keepdims=True))
-    norm[0] = root[0, 0]
-    norm[1] = root[1, 0]
+    total = total_in[...]
+    lane = lax.broadcasted_iota(jnp.int32, total.shape, 1)
+    for n, (part, cells) in enumerate(((lane < 64, count), (lane >= 64, 3.0 * count))):
+        root = jnp.sqrt(jnp.sum(jnp.where(part, total, 0.0), axis=1, keepdims=True) * (1.0 / cells))
+        norm[n] = root[0, 0]
     copies.append(pltpu.make_async_copy(norm, norm_out, sems.at[2]))
     copies[2].start()
     for copy in copies:
@@ -532,7 +578,7 @@
         out_shape=(
             pltpu.VMEM(chi_field.shape, jnp.float32),
             pltpu.VMEM(gamma_field.shape, jnp.float32),
-            pltpu.VMEM((8, 128), jnp.float32),
+            pltpu.VMEM((1, 128), jnp.float32),
         ),
         in_specs=[pl.BlockSpec(memory_space=pltpu.HBM)] * 6,
         out_specs=(vmem, vmem, vmem),
@@ -541,7 +587,7 @@
             pltpu.VMEM(block, jnp.float32),
         ]
         + [pltpu.VMEM((cx, cy, cz), jnp.float32)] * 3
-        + [pltpu.VMEM((4, cy, cz), jnp.float32)] * 3
+        + [pltpu.VMEM((2, 4, cy, cz), jnp.float32)] * 3
         + [
             pltpu.VMEM((GEO, cx) + block[1:], jnp.float32),
             pltpu.VMEM((2, 8, 128), jnp.float32),
@@ -553,7 +599,8 @@
         + [pltpu.VMEM((GEO, cx, cy, cz), jnp.float32)] * 4
         + [pltpu.VMEM((2, cx * cy, cz), jnp.bfloat16)] * 3
         + [pltpu.VMEM((n, 8, 128), jnp.float32) for n in (sizes[0], sizes[1] * sizes[2])]
-        + [dma((n,)) for n in (7, 6, 6, 4, 4, 2, 2, 4, 4, 2, 2, 2, 2)]
+        + [dma((n,)) for n in (7, 6, 6, 4, 4, 2, 2, 8, 8, 2, 2)]
+        + [dma((2, 2))] * 2
         + [dma((n,)) for n in (sizes[0], sizes[1] * sizes[2], 2) for _ in range(2)],
         compiler_params=pltpu.CompilerParams(
             collective_id=0, has_side_effects=True, vmem_limit_bytes=67043328 - 16 * chi_field.size - 16384

time: 34.4 us -> 32.8 us (0.953)
  Pallas kernels: 33.6 us -> 32 us
    pallas_call x1, Pallas kernels: 32.8 us -> 31.2 us  [on_device(): pl.pallas_call(functools.partial(kernel, sizes), out_shape=(pltpu.VMEM(ch...]
where the time goes in v3:
time: 32.8 us; the launch traced here: 32.6 us
  Pallas kernels  32 us (98%)
  between operations  0.64 us (2%)
    pallas_call x1, Pallas kernels, on_device(): pl.pallas_call(functools.partial(kernel, sizes), out_shape=(pltpu.VMEM(ch...  31.2 us
    pallas_call x1, Pallas kernels, on_device(): pl.pallas_call(functools.partial(deliver, count), out_shape=(jax.ShapeDty...  0.82 us

profile of v3, /device:TPU:0, one launch (start us, length us, event | category | flops | bytes accessed | tf_op | source)
XLA Modules:
  0.0 32.6 jit_solution(8635424232735960073)
XLA Ops:
  0.6 31.2 %shard_map.85 = (f32[8,32,128]{2,1,0:T(8,128)S(1)}, f32[3,8,32,128]{3,2,1,0:T(8,128)S(1)}, f32[1,128]{1,0:T(1,128)S(1)}) custom-call(f32[8,32,128]{2,1,0:T(8,128)} %chi_in.1, f32[6,8,32,128]{3,2,1,0:T(8,128)} %met_in.1, f32[6,8,32,128]{3,2,1,0:T(8,128)} %curv_in.1, f32[8,32,128]{2,1,0:T(8,128)} %trk_in.1, f32[3,8,32,128]{3,2,1,0:T(8,128)} %gam_in.1, ...), custom_call_target="tpu_custom_call" | custom-call | tf_op jit(solution)/shard_map/pallas_call | solution.py:576
  31.8 0.8 %shard_map.86 = (f32[8,32,128]{2,1,0:T(8,128)}, f32[3,8,32,128]{3,2,1,0:T(8,128)}, f32[2]{0:T(128)}) custom-call(f32[8,32,128]{2,1,0:T(8,128)S(1)} %get-tuple-element.6.ham_in, f32[3,8,32,128]{3,2,1,0:T(8,128)S(1)} %get-tuple-element.7.mom_in, f32[1,128]{1,0:T(1,128)S(1)} %get-tuple-element.8.total_in), custom_call_target="tpu_custom_call" | custom-call | tf_op jit(solution)/shard_map/pallas_call | solution.py:610

commit v4 on v3

--- a/solution.py
+++ b/solution.py
@@ -185,9 +185,9 @@
     ham_out, mom_out, total_out,
     cells, packed, pack_own, pack_left, pack_right, edge_own, edge_left, edge_right, slope, sums,
     part_out, part, weights, z_one, z_two, y_one, yz_two, xz_two, mid_split, dy_split, dx_split,
-    slots_x, slots_y,
+    slots_x,
     load_sem, xs, xr, ys, yr, zs, zr, es, er, pys, pyr, ezs, ezr,
-    rxs, rxr, rys, ryr, cs, cr,
+    rxs, rxr, cs, cr, ready,
 ):
     nx, ny, nz = sizes
     cx, cy = chi_in.shape[0], chi_in.shape[1]
@@ -236,6 +236,9 @@
         for step in hops(axes):
             pl.semaphore_signal(barrier, inc=1, device_id=peer(axes, step), device_id_type=MESH)
     pl.semaphore_wait(barrier, ny * nz + nx - 2)
+
+    for step in hops((1, 2)):
+        pl.semaphore_signal(ready, inc=1, device_id=peer((1, 2), step), device_id_type=MESH)
 
     def send(src, dst, send_sem, recv_sem, axis, step):
         copy = pltpu.make_async_remote_copy(
@@ -529,11 +532,12 @@
     folded = [sums[n] + pltpu.roll(sums[n], 64, 1) for n in range(2)]
     total = jnp.sum(jnp.where(lane < 64, folded[0], folded[1]), axis=0, keepdims=True)
     line = pl.ds(0, 1)
+    pl.semaphore_wait(ready, ny * nz - 1)
     pending = []
-    for axes, slots, ss, rs in (((1, 2), slots_y, rys, ryr), ((0,), slots_x, rxs, rxr)):
+    for axes, slots, ss, rs in (((0, 1, 2), slots_x, rxs, rxr),):
         here = place_in(axes)
         slots[here, line] = total
-        others = hops(axes)
+        others = sorted(hops(axes), key=lambda step: -sum(min(a, b - a) for a, b in zip(step, sizes)))
         for n, step in enumerate(others):
             pending.append(send(slots.at[here, line], slots.at[here, line], ss.at[n], rs.at[here], axes, step))
         for n, step in enumerate(others):
@@ -598,10 +602,11 @@
         ]
         + [pltpu.VMEM((GEO, cx, cy, cz), jnp.float32)] * 4
         + [pltpu.VMEM((2, cx * cy, cz), jnp.bfloat16)] * 3
-        + [pltpu.VMEM((n, 8, 128), jnp.float32) for n in (sizes[0], sizes[1] * sizes[2])]
+        + [pltpu.VMEM((n, 8, 128), jnp.float32) for n in (np.prod(sizes),)]
         + [dma((n,)) for n in (7, 6, 6, 4, 4, 2, 2, 8, 8, 2, 2)]
         + [dma((2, 2))] * 2
-        + [dma((n,)) for n in (sizes[0], sizes[1] * sizes[2], 2) for _ in range(2)],
+        + [dma((n,)) for n in (np.prod(sizes), 2) for _ in range(2)]
+        + [pltpu.SemaphoreType.REGULAR],
         compiler_params=pltpu.CompilerParams(
             collective_id=0, has_side_effects=True, vmem_limit_bytes=67043328 - 16 * chi_field.size - 16384
         ),

time: 32.8 us -> 31.2 us (0.951)
  Pallas kernels: 32 us -> 30.4 us
    pallas_call x1, Pallas kernels: 31.2 us -> 29.5 us  [on_device(): pl.pallas_call(functools.partial(kernel, sizes), out_shape=(pltpu.VMEM(ch...]
where the time goes in v4:
time: 31.2 us; the launch traced here: 31 us
  Pallas kernels  30.4 us (97%)
  between operations  0.64 us (2%)
    pallas_call x1, Pallas kernels, on_device(): pl.pallas_call(functools.partial(kernel, sizes), out_shape=(pltpu.VMEM(ch...  29.5 us
    pallas_call x1, Pallas kernels, on_device(): pl.pallas_call(functools.partial(deliver, count), out_shape=(jax.ShapeDty...  0.82 us

profile of v4, /device:TPU:0, one launch (start us, length us, event | category | flops | bytes accessed | tf_op | source)
XLA Modules:
  0.0 31.0 jit_solution(8482676638719550653)
XLA Ops:
  0.6 29.5 %shard_map.85 = (f32[8,32,128]{2,1,0:T(8,128)S(1)}, f32[3,8,32,128]{3,2,1,0:T(8,128)S(1)}, f32[1,128]{1,0:T(1,128)S(1)}) custom-call(f32[8,32,128]{2,1,0:T(8,128)} %chi_in.1, f32[6,8,32,128]{3,2,1,0:T(8,128)} %met_in.1, f32[6,8,32,128]{3,2,1,0:T(8,128)} %curv_in.1, f32[8,32,128]{2,1,0:T(8,128)} %trk_in.1, f32[3,8,32,128]{3,2,1,0:T(8,128)} %gam_in.1, ...), custom_call_target="tpu_custom_call" | custom-call | tf_op jit(solution)/shard_map/pallas_call | solution.py:580
  30.2 0.8 %shard_map.86 = (f32[8,32,128]{2,1,0:T(8,128)}, f32[3,8,32,128]{3,2,1,0:T(8,128)}, f32[2]{0:T(128)}) custom-call(f32[8,32,128]{2,1,0:T(8,128)S(1)} %get-tuple-element.6.ham_in, f32[3,8,32,128]{3,2,1,0:T(8,128)S(1)} %get-tuple-element.7.mom_in, f32[1,128]{1,0:T(1,128)S(1)} %get-tuple-element.8.total_in), custom_call_target="tpu_custom_call" | custom-call | tf_op jit(solution)/shard_map/pallas_call | solution.py:615

commit v5 on v4

--- a/solution.py
+++ b/solution.py
@@ -12,6 +12,7 @@
 MESH = pl.DeviceIdType.MESH
 GX, CHI, MET, CURV, TRK, GY, GZ = 0, 1, 2, 8, 14, 15, 16
 GEO = 7
+X_MET, X_CHI, X_GX, Y_GEO, Y_REST, Y_PACK, Z_PACK, EDGE_Y, EDGE_Z, PART, NORM = range(11)
 Z_FIELDS = tuple(range(CHI, GY)) + (GZ,)
 TOP = 8
 
@@ -183,11 +184,9 @@
     sizes,
     chi_in, met_in, curv_in, trk_in, gam_in, weights_in,
     ham_out, mom_out, total_out,
-    cells, packed, pack_own, pack_left, pack_right, edge_own, edge_left, edge_right, slope, sums,
+    cells, packed, pack_own, pack_in, edge_own, edge_in, slope, sums,
     part_out, part, weights, z_one, z_two, y_one, yz_two, xz_two, mid_split, dy_split, dx_split,
-    slots_x,
-    load_sem, xs, xr, ys, yr, zs, zr, es, er, pys, pyr, ezs, ezr,
-    rxs, rxr, cs, cr, ready,
+    slots, load_sem, sent, got, ready,
 ):
     nx, ny, nz = sizes
     cx, cy = chi_in.shape[0], chi_in.shape[1]
@@ -217,16 +216,14 @@
     own_x, own_y = pl.ds(2, cx), pl.ds(TOP, cy)
     loads = [
         pltpu.make_async_copy(src, dst, load_sem.at[n])
-        for n, (src, dst) in enumerate(
-            (
-                (met_in, cells.at[pl.ds(MET, 6), own_x, own_y]),
-                (chi_in, cells.at[CHI, own_x, own_y]),
-                (gam_in.at[0], cells.at[GX, own_x, own_y]),
-                (curv_in, cells.at[pl.ds(CURV, 6), own_x, own_y]),
-                (trk_in, cells.at[TRK, own_x, own_y]),
-                (gam_in.at[pl.ds(1, 2)], cells.at[pl.ds(GY, 2), own_x, own_y]),
-                (weights_in, weights),
-            )
+        for n, src, dst in (
+            (0, met_in, cells.at[pl.ds(MET, 6), own_x, own_y]),
+            (1, chi_in, cells.at[CHI, own_x, own_y]),
+            (1, gam_in.at[0], cells.at[GX, own_x, own_y]),
+            (2, curv_in, cells.at[pl.ds(CURV, 6), own_x, own_y]),
+            (2, trk_in, cells.at[TRK, own_x, own_y]),
+            (2, gam_in.at[pl.ds(1, 2)], cells.at[pl.ds(GY, 2), own_x, own_y]),
+            (3, weights_in, weights),
         )
     ]
     for copy in loads[:6]:
@@ -240,44 +237,57 @@
     for step in hops((1, 2)):
         pl.semaphore_signal(ready, inc=1, device_id=peer((1, 2), step), device_id_type=MESH)
 
-    def send(src, dst, send_sem, recv_sem, axis, step):
-        copy = pltpu.make_async_remote_copy(
-            src_ref=src, dst_ref=dst, send_sem=send_sem, recv_sem=recv_sem,
-            device_id=peer(axis, step), device_id_type=MESH,
+    def loaded(n, ref):
+        pltpu.make_async_copy(ref, ref, load_sem.at[n]).wait()
+
+    def copy_to(src, dst, n, axes, step):
+        return pltpu.make_async_remote_copy(
+            src_ref=src, dst_ref=dst, send_sem=sent.at[n], recv_sem=got.at[n],
+            device_id=peer(axes, step), device_id_type=MESH,
         )
-        copy.start()
-        return copy
+
+    def send(src, dst, n, axes, step):
+        copy_to(src, dst, n, axes, step).start()
 
     low_x, high_x = pl.ds(2, 2), pl.ds(cx, 2)
     before_x, after_x = pl.ds(0, 2), pl.ds(cx + 2, 2)
     low_y, high_y = pl.ds(TOP, 2), pl.ds(TOP + cy - 2, 2)
     before_y, after_y = pl.ds(TOP - 2, 2), pl.ds(TOP + cy, 2)
-    x_faces, y_faces = [], []
-
-    def send_x(fields):
-        n = len(x_faces)
-        x_faces.extend((
-            send(cells.at[fields, high_x, own_y], cells.at[fields, before_x, own_y], xs.at[n], xr.at[n], 0, 1),
-            send(cells.at[fields, low_x, own_y], cells.at[fields, after_x, own_y], xs.at[n + 1], xr.at[n + 1], 0, -1),
-        ))
-
-    def send_y(fields):
-        n = len(y_faces)
-        y_faces.extend((
-            send(cells.at[fields, own_x, high_y], cells.at[fields, own_x, before_y], ys.at[n], yr.at[n], 1, 1),
-            send(cells.at[fields, own_x, low_y], cells.at[fields, own_x, after_y], ys.at[n + 1], yr.at[n + 1], 1, -1),
-        ))
-
-    loads[0].wait()
-    send_x(pl.ds(MET, 6))
-    loads[1].wait()
-    send_x(pl.ds(CHI, 1))
-    send_y(pl.ds(CHI, GEO))
-    loads[2].wait()
-    send_x(pl.ds(GX, 1))
-    for copy in loads[3:6]:
-        copy.wait()
-    send_y(pl.ds(CURV, 8))
+    geo = pl.ds(CHI, GEO)
+    several = nz > 2
+    bulk = {
+        X_MET: cells.at[pl.ds(MET, 6), pl.ds(0, 4), own_y],
+        X_CHI: cells.at[pl.ds(CHI, 1), pl.ds(0, 4), own_y],
+        X_GX: cells.at[pl.ds(GX, 1), pl.ds(0, 4), own_y],
+        Y_GEO: cells.at[geo, own_x, pl.ds(0, 4)],
+        Y_REST: cells.at[pl.ds(CURV, 8), own_x, pl.ds(0, 4)],
+        Y_PACK: packed.at[own_x, pl.ds(0, 4)],
+        Z_PACK: pack_in if several else pack_in.at[0],
+        EDGE_Y: cells.at[geo, pl.ds(0, 4), pl.ds(0, 4)],
+        EDGE_Z: edge_in if several else edge_in.at[0],
+        PART: part,
+        NORM: slots.at[pl.ds(0, nx * ny * nz - 1)],
+    }
+
+    def wait_for(n):
+        copy_to(bulk[n], bulk[n], n, 0, 1).wait_recv()
+
+    def send_x(fields, n):
+        send(cells.at[fields, high_x, own_y], cells.at[fields, before_x, own_y], n, 0, 1)
+        send(cells.at[fields, low_x, own_y], cells.at[fields, after_x, own_y], n, 0, -1)
+
+    def send_y(fields, n, layers=own_x):
+        send(cells.at[fields, layers, high_y], cells.at[fields, layers, before_y], n, 1, 1)
+        send(cells.at[fields, layers, low_y], cells.at[fields, layers, after_y], n, 1, -1)
+
+    loaded(0, cells.at[pl.ds(MET, 6), own_x, own_y])
+    send_x(pl.ds(MET, 6), X_MET)
+    loaded(1, cells.at[pl.ds(GX, 2), own_x, own_y])
+    send_x(pl.ds(CHI, 1), X_CHI)
+    send_y(geo, Y_GEO)
+    send_x(pl.ds(GX, 1), X_GX)
+    loaded(2, cells.at[pl.ds(CURV, 9), own_x, own_y])
+    send_y(pl.ds(CURV, 8), Y_REST)
     loads[6].start()
 
     tiles = cy // 8
@@ -301,38 +311,34 @@
 
     packing(Z_FIELDS, pack_own, lambda at: at + 2)
 
-    def send_z(own, left, right, send_sem, recv_sem):
-        faces = [send(own, left, send_sem.at[0], recv_sem.at[0], 2, 1)]
-        if nz > 2:
-            faces.append(send(own, right, send_sem.at[1], recv_sem.at[1], 2, -1))
-        return faces
-
-    def joined(left, right, at):
-        return jnp.where(far_side, right[at], left[at]) if nz > 2 else left[at]
-
-    z_faces = send_z(pack_own, pack_left, pack_right, zs, zr)
+    def send_z(own, target, n):
+        send(own, target(0), n, 2, 1)
+        if several:
+            send(own, target(1), n, 2, -1)
+
+    def joined(both):
+        return jnp.where(far_side, both(1), both(0)) if several else both(0)
+
+    send_z(pack_own, lambda side: pack_in.at[side], Z_PACK)
     sums[...] = jnp.zeros_like(sums)
     missing = jnp.zeros((7, 2, cy, 128), jnp.float32)
     cells[pl.ds(CURV, 7), before_x, own_y] = missing
     cells[pl.ds(CURV, 7), after_x, own_y] = missing
-    for copy in z_faces:
-        copy.wait_recv()
+    wait_for(Z_PACK)
 
     def keep_split(target, value, at=0):
         for n, half in enumerate(split(value)):
             target[n, pl.ds(at, value.shape[0])] = half
 
     def merge(x, carry):
-        value = joined(pack_left, pack_right, x)
+        value = joined(lambda side: pack_in[side, x])
         packed[x + 2, own_y] = value
         keep_split(mid_split, value, pl.multiple_of(x * cy, cy))
         return carry
 
     lax.fori_loop(0, cx, merge, 0)
-    py_faces = [
-        send(packed.at[own_x, high_y], packed.at[own_x, before_y], pys.at[0], pyr.at[0], 1, 1),
-        send(packed.at[own_x, low_y], packed.at[own_x, after_y], pys.at[1], pyr.at[1], 1, -1),
-    ]
+    send(packed.at[own_x, high_y], packed.at[own_x, before_y], Y_PACK, 1, 1)
+    send(packed.at[own_x, low_y], packed.at[own_x, after_y], Y_PACK, 1, -1)
     loads[6].wait()
     flat = (cx * cy, 128)
 
@@ -448,15 +454,13 @@
     rises(((8, cy - 16),))
     slopes(((2, cx - 4),))
     run(*inner, *middle, True)
-    for copy in y_faces[:2] + py_faces:
-        copy.wait_recv()
+    wait_for(Y_GEO)
+    wait_for(Y_PACK)
     rises(((0, 8), (cy - 8, 8)))
     rims(((2, cx - 4),))
-    for copy in y_faces[2:]:
-        copy.wait_recv()
+    wait_for(Y_REST)
     run(*inner, *rim, True)
-    for copy in x_faces[:2]:
-        copy.wait_recv()
+    wait_for(X_MET)
 
     def offer(t, carry):
         rows = pl.ds(pl.multiple_of(TOP + t * 8, 8), 8)
@@ -477,45 +481,28 @@
         return carry
 
     lax.fori_loop(0, tiles, offer, 0)
-    part_faces = [
-        send(part_out.at[0], part.at[:, pl.ds(2, 2)], cs.at[0], cr.at[0], 0, -1),
-        send(part_out.at[1], part.at[:, pl.ds(0, 2)], cs.at[1], cr.at[1], 0, 1),
-    ]
-    edges, edge_z = [], []
-
-    def relay(fields):
+    send(part_out.at[0], part.at[:, pl.ds(2, 2)], PART, 0, -1)
+    send(part_out.at[1], part.at[:, pl.ds(0, 2)], PART, 0, 1)
+
+    def relay(n, fields, sliced):
         for layers in (before_x, after_x):
-            n = len(edges)
-            edges.extend((
-                send(cells.at[fields, layers, high_y], cells.at[fields, layers, before_y], es.at[n], er.at[n], 1, 1),
-                send(cells.at[fields, layers, low_y], cells.at[fields, layers, after_y], es.at[n + 1], er.at[n + 1], 1, -1),
-            ))
-
-    def relay_z(fields):
-        n = len(edge_z)
+            send_y(sliced, EDGE_Y, layers)
         packing(fields, edge_own.at[n], lambda at: at + at // 2 * cx)
-        edge_z.append(send_z(edge_own.at[n], edge_left.at[n], edge_right.at[n], ezs.at[n], ezr.at[n]))
-
-    relay(pl.ds(MET, 6))
-    relay_z((None,) + tuple(range(MET, CURV)))
-    for copy in x_faces[2:4]:
-        copy.wait_recv()
-    relay(pl.ds(CHI, 1))
-    relay_z((CHI,))
-    for copy in edge_z[0] + edge_z[1]:
-        copy.wait_recv()
+        send_z(edge_own.at[n], lambda side: edge_in.at[side, n], EDGE_Z)
+
+    relay(0, (None,) + tuple(range(MET, CURV)), pl.ds(MET, 6))
+    wait_for(X_CHI)
+    relay(1, (CHI,), pl.ds(CHI, 1))
+    wait_for(EDGE_Z)
     for at in range(4):
-        packed[at + at // 2 * cx, own_y] = joined(edge_left.at[0], edge_right.at[0], at) + joined(edge_left.at[1], edge_right.at[1], at)
+        packed[at + at // 2 * cx, own_y] = joined(lambda side: edge_in[side, 0, at] + edge_in[side, 1, at])
     slopes(((0, 2), (cx - 2, 2)))
-    for copy in x_faces[4:]:
-        copy.wait_recv()
+    wait_for(X_GX)
     run(*outer, *middle, False)
-    for copy in edges:
-        copy.wait_recv()
+    wait_for(EDGE_Y)
     rims(((0, 2), (cx - 2, 2)))
     run(*outer, *rim, False)
-    for copy in part_faces:
-        copy.wait_recv()
+    wait_for(PART)
 
     def finish(n, carry):
         at, rows = n // tiles, pl.ds(pl.multiple_of(lax.rem(n, tiles) * 8, 8), 8)
@@ -531,25 +518,16 @@
     lane = lax.broadcasted_iota(jnp.int32, (8, 128), 1)
     folded = [sums[n] + pltpu.roll(sums[n], 64, 1) for n in range(2)]
     total = jnp.sum(jnp.where(lane < 64, folded[0], folded[1]), axis=0, keepdims=True)
-    line = pl.ds(0, 1)
     pl.semaphore_wait(ready, ny * nz - 1)
-    pending = []
-    for axes, slots, ss, rs in (((0, 1, 2), slots_x, rxs, rxr),):
-        here = place_in(axes)
-        slots[here, line] = total
-        others = sorted(hops(axes), key=lambda step: -sum(min(a, b - a) for a, b in zip(step, sizes)))
-        for n, step in enumerate(others):
-            pending.append(send(slots.at[here, line], slots.at[here, line], ss.at[n], rs.at[here], axes, step))
-        for n, step in enumerate(others):
-            source = place_in(axes, step)
-            pltpu.make_async_remote_copy(
-                src_ref=slots.at[source, line], dst_ref=slots.at[source, line], send_sem=ss.at[n],
-                recv_sem=rs.at[source], device_id=peer(axes, step), device_id_type=MESH,
-            ).wait_recv()
-        total = total_of(slots[n, line] for n in range(len(others) + 1))
-    total_out[...] = total
-    for copy in x_faces + y_faces + z_faces + py_faces + edges + edge_z[0] + edge_z[1] + part_faces + pending:
-        copy.wait_send()
+    axes = (0, 1, 2)
+    here = pl.ds(place_in(axes), 1)
+    slots[here] = total
+    for step in sorted(hops(axes), key=lambda step: -sum(min(a, b - a) for a, b in zip(step, sizes))):
+        send(slots.at[here], slots.at[here], NORM, axes, step)
+    wait_for(NORM)
+    total_out[...] = jnp.sum(slots[...], axis=0, keepdims=True)
+    for n, ref in bulk.items():
+        copy_to(ref, ref, n, 0, 1).wait_send()
 
 
 def deliver(count, ham_in, mom_in, total_in, ham_out, mom_out, norm_out, norm, sems):
@@ -590,8 +568,7 @@
             pltpu.VMEM((17,) + block, jnp.float32),
             pltpu.VMEM(block, jnp.float32),
         ]
-        + [pltpu.VMEM((cx, cy, cz), jnp.float32)] * 3
-        + [pltpu.VMEM((2, 4, cy, cz), jnp.float32)] * 3
+        + [pltpu.VMEM(shape + (cy, cz), jnp.float32) for shape in ((cx,), (2, cx), (2, 4), (2, 2, 4))]
         + [
             pltpu.VMEM((GEO, cx) + block[1:], jnp.float32),
             pltpu.VMEM((2, 8, 128), jnp.float32),
@@ -602,10 +579,7 @@
         ]
         + [pltpu.VMEM((GEO, cx, cy, cz), jnp.float32)] * 4
         + [pltpu.VMEM((2, cx * cy, cz), jnp.bfloat16)] * 3
-        + [pltpu.VMEM((n, 8, 128), jnp.float32) for n in (np.prod(sizes),)]
-        + [dma((n,)) for n in (7, 6, 6, 4, 4, 2, 2, 8, 8, 2, 2)]
-        + [dma((2, 2))] * 2
-        + [dma((n,)) for n in (np.prod(sizes), 2) for _ in range(2)]
+        + [pltpu.VMEM((np.prod(sizes), 128), jnp.float32), dma((4,)), dma((11,)), dma((11,))]
         + [pltpu.SemaphoreType.REGULAR],
         compiler_params=pltpu.CompilerParams(
             collective_id=0, has_side_effects=True, vmem_limit_bytes=67043328 - 16 * chi_field.size - 16384

time: 31.2 us -> 30.2 us (0.968)
  Pallas kernels: 30.4 us -> 29.4 us
    pallas_call x1, Pallas kernels: 29.5 us -> 28.6 us  [on_device(): pl.pallas_call(functools.partial(kernel, sizes), out_shape=(pltpu.VMEM(ch...]
where the time goes in v5:
time: 30.2 us; the launch traced here: 30 us
  Pallas kernels  29.4 us (97%)
  between operations  0.64 us (2%)
    pallas_call x1, Pallas kernels, on_device(): pl.pallas_call(functools.partial(kernel, sizes), out_shape=(pltpu.VMEM(ch...  28.6 us
    pallas_call x1, Pallas kernels, on_device(): pl.pallas_call(functools.partial(deliver, count), out_shape=(jax.ShapeDty...  0.82 us

profile of v5, /device:TPU:0, one launch (start us, length us, event | category | flops | bytes accessed | tf_op | source)
XLA Modules:
  0.0 30.0 jit_solution(18305519099756532717)
XLA Ops:
  0.6 28.6 %shard_map.85 = (f32[8,32,128]{2,1,0:T(8,128)S(1)}, f32[3,8,32,128]{3,2,1,0:T(8,128)S(1)}, f32[1,128]{1,0:T(1,128)S(1)}) custom-call(f32[8,32,128]{2,1,0:T(8,128)} %chi_in.1, f32[6,8,32,128]{3,2,1,0:T(8,128)} %met_in.1, f32[6,8,32,128]{3,2,1,0:T(8,128)} %curv_in.1, f32[8,32,128]{2,1,0:T(8,128)} %trk_in.1, f32[3,8,32,128]{3,2,1,0:T(8,128)} %gam_in.1, ...), custom_call_target="tpu_custom_call" | custom-call | tf_op jit(solution)/shard_map/pallas_call | solution.py:558
  29.2 0.8 %shard_map.86 = (f32[8,32,128]{2,1,0:T(8,128)}, f32[3,8,32,128]{3,2,1,0:T(8,128)}, f32[2]{0:T(128)}) custom-call(f32[8,32,128]{2,1,0:T(8,128)S(1)} %get-tuple-element.6.ham_in, f32[3,8,32,128]{3,2,1,0:T(8,128)S(1)} %get-tuple-element.7.mom_in, f32[1,128]{1,0:T(1,128)S(1)} %get-tuple-element.8.total_in), custom_call_target="tpu_custom_call" | custom-call | tf_op jit(solution)/shard_map/pallas_call | solution.py:589

commit v6 on v5

--- a/solution.py
+++ b/solution.py
@@ -80,7 +80,7 @@
     return [m * scale for m in (m00, m01, m02, m11, m12, m22)]
 
 
-def cell_math(load, load_dx, load_dy, load_z, load_zz, load_xz, load_yz):
+def cell_math(load, load_dx, load_dy, load_z, load_zz, load_xz, load_yz, whole):
     zpos = {f: n for n, f in enumerate(Z_FIELDS)}
     gu = inverse([load(MET + n, 0, 0) for n in range(6)])
     gu_hess = [12.0 * gu[n] if n in (0, 3, 5) else 2.0 * gu[n] for n in range(6)]
@@ -94,11 +94,11 @@
         dy, dz = load_dy(n), load_z(n)
         dxx = second(xs[0], xs[1], c, xs[2], xs[3])
         dyy = second(ys[0], ys[1], c, ys[2], ys[3])
-        dzz = load_zz(n)
-        dxy = first(*(load_dx(n, s) for s in (-2, -1, 1, 2)))
-        dxz, dyz = load_xz(n), load_yz(n)
-        hess = (dxx, dxy, dxz, dyy, dyz, dzz)
-        return (dx, dy, dz), total_of(gu_hess[n] * hess[n] for n in range(6))
+        hess = {0: dxx, 3: dyy, 4: load_yz(n), 5: load_zz(n)}
+        if whole:
+            hess[1] = first(*(load_dx(n, s) for s in (-2, -1, 1, 2)))
+            hess[2] = load_xz(n)
+        return (dx, dy, dz), total_of(gu_hess[k] * hess[k] for k in sorted(hess))
 
     chi = load(CHI, 0, 0)
     dchi, chi_box = geo(CHI)
@@ -151,7 +151,9 @@
     def dz_of(f):
         return load_z(zpos[f])
 
-    div = dx_of(GX) + dy_of(GY) + dz_of(GZ)
+    div = dy_of(GY) + dz_of(GZ)
+    if whole:
+        div = dx_of(GX) + div
     inv_chi = 1.0 / chi
     curv = [load(CURV + n, 0, 0) for n in range(6)]
     mixed = [
@@ -272,13 +274,32 @@
     def wait_for(n):
         copy_to(bulk[n], bulk[n], n, 0, 1).wait_recv()
 
+    def each_way(axis, ahead, back):
+        odd = lax.rem(me[axis], 2) == 1
+
+        @pl.when(odd)
+        def _():
+            ahead()
+            back()
+
+        @pl.when(jnp.logical_not(odd))
+        def _():
+            back()
+            ahead()
+
     def send_x(fields, n):
-        send(cells.at[fields, high_x, own_y], cells.at[fields, before_x, own_y], n, 0, 1)
-        send(cells.at[fields, low_x, own_y], cells.at[fields, after_x, own_y], n, 0, -1)
+        each_way(
+            0,
+            lambda: send(cells.at[fields, high_x, own_y], cells.at[fields, before_x, own_y], n, 0, 1),
+            lambda: send(cells.at[fields, low_x, own_y], cells.at[fields, after_x, own_y], n, 0, -1),
+        )
 
     def send_y(fields, n, layers=own_x):
-        send(cells.at[fields, layers, high_y], cells.at[fields, layers, before_y], n, 1, 1)
-        send(cells.at[fields, layers, low_y], cells.at[fields, layers, after_y], n, 1, -1)
+        each_way(
+            1,
+            lambda: send(cells.at[fields, layers, high_y], cells.at[fields, layers, before_y], n, 1, 1),
+            lambda: send(cells.at[fields, layers, low_y], cells.at[fields, layers, after_y], n, 1, -1),
+        )
 
     loaded(0, cells.at[pl.ds(MET, 6), own_x, own_y])
     send_x(pl.ds(MET, 6), X_MET)
@@ -294,7 +315,7 @@
     group = lax.shift_right_logical(lax.broadcasted_iota(jnp.int32, (8, 128), 1), 2)
     far_side = (lax.broadcasted_iota(jnp.int32, (cy, 128), 1) & 2) != 0
 
-    def packing(fields, target, layer):
+    def packing(fields, target, layer, unroll):
         def pack(step, carry):
             at, y = step // tiles, lax.rem(step, tiles) * 8
             rows = pl.ds(pl.multiple_of(TOP + y, 8), 8)
@@ -307,9 +328,9 @@
             target[at, pl.ds(pl.multiple_of(y, 8), 8)] = total_of(picked)
             return carry
 
-        lax.fori_loop(0, target.shape[0] * tiles, pack, 0, unroll=4)
-
-    packing(Z_FIELDS, pack_own, lambda at: at + 2)
+        lax.fori_loop(0, target.shape[0] * tiles, pack, 0, unroll=unroll)
+
+    packing(Z_FIELDS, pack_own, lambda at: at + 2, 4)
 
     def send_z(own, target, n):
         send(own, target(0), n, 2, 1)
@@ -383,6 +404,16 @@
 
         lax.fori_loop(0, GEO, one, 0, unroll=7)
 
+    def climbs(pieces, fields):
+        def one(n, carry):
+            for base, count in pieces:
+                slope[n, pl.ds(base, count), own_y] = first(
+                    *(cells[n + CHI, pl.ds(base + 2 + s, count), own_y] for s in (-2, -1, 1, 2))
+                )
+            return carry
+
+        lax.fori_loop(*fields, one, 0, unroll=fields[1] - fields[0])
+
     def slopes(pieces):
         rows = [count * cy for _, count in pieces]
         at = 0
@@ -393,11 +424,7 @@
         total = at
 
         def one(n, carry):
-            values = []
-            for (base, count), size in zip(pieces, rows):
-                dx = first(*(cells[n + CHI, pl.ds(base + 2 + s, count), own_y] for s in (-2, -1, 1, 2)))
-                slope[n, pl.ds(base, count), own_y] = dx
-                values.append(dx.reshape(size, 128))
+            values = [slope[n, pl.ds(base, count), own_y].reshape(size, 128) for (base, count), size in zip(pieces, rows)]
             both = along_z(jnp.concatenate(values, 0), dx_split[:, :total], weights[n, :, :128])
             at = 0
             for (base, count), size in zip(pieces, rows):
@@ -407,7 +434,7 @@
 
         lax.fori_loop(0, GEO, one, 0, unroll=7)
 
-    def tile_at(x, y):
+    def tile_at(x, y, whole):
         rows = pl.ds(pl.multiple_of(y, 8), 8)
         ham, momentum = cell_math(
             lambda f, sx, sy: cells[f, x + 2 + sx, pl.ds(TOP + y + sy, 8)],
@@ -417,12 +444,14 @@
             lambda n: z_two[n, x, rows],
             lambda n: xz_two[n, x, rows],
             lambda n: yz_two[n, x, rows],
+            whole,
         )
         ham_out[x, rows] = ham
         for i in range(3):
             mom_out[i, x, rows] = momentum[i]
-        sums[0] += ham * ham
-        return momentum
+        if whole:
+            sums[0] += ham * ham
+            sums[1] += momentum[0] * momentum[0] + momentum[1] * momentum[1] + momentum[2] * momentum[2]
 
     def rims(pieces):
         def one(n, carry):
@@ -438,20 +467,20 @@
     def outer_x(at):
         return at + at // 2 * (cx - 4)
 
-    def run(layers, layer, count, row, square):
+    def run(layers, layer, count, row, whole):
         def one(n, carry):
-            momentum = tile_at(layer(n // count), row(lax.rem(n, count)))
-            if square:
-                sums[1] += momentum[0] * momentum[0] + momentum[1] * momentum[1] + momentum[2] * momentum[2]
+            tile_at(layer(n // count), row(lax.rem(n, count)), whole)
             return carry
 
         lax.fori_loop(0, layers * count, one, 0)
 
     inner = (cx - 4, lambda at: at + 2)
     outer = (4, outer_x)
+    every = (tiles, lambda at: 8 * at)
     middle = (tiles - 2, lambda at: 8 * at + 8)
     rim = (2, lambda at: at * (cy - 8))
     rises(((8, cy - 16),))
+    climbs(((2, cx - 4),), (0, GEO))
     slopes(((2, cx - 4),))
     run(*inner, *middle, True)
     wait_for(Y_GEO)
@@ -481,27 +510,52 @@
         return carry
 
     lax.fori_loop(0, tiles, offer, 0)
-    send(part_out.at[0], part.at[:, pl.ds(2, 2)], PART, 0, -1)
-    send(part_out.at[1], part.at[:, pl.ds(0, 2)], PART, 0, 1)
-
-    def relay(n, fields, sliced):
+    each_way(
+        0,
+        lambda: send(part_out.at[1], part.at[:, pl.ds(0, 2)], PART, 0, 1),
+        lambda: send(part_out.at[0], part.at[:, pl.ds(2, 2)], PART, 0, -1),
+    )
+
+    def relay(n, fields, sliced, unroll):
         for layers in (before_x, after_x):
             send_y(sliced, EDGE_Y, layers)
-        packing(fields, edge_own.at[n], lambda at: at + at // 2 * cx)
+        packing(fields, edge_own.at[n], lambda at: at + at // 2 * cx, unroll)
         send_z(edge_own.at[n], lambda side: edge_in.at[side, n], EDGE_Z)
 
-    relay(0, (None,) + tuple(range(MET, CURV)), pl.ds(MET, 6))
+    ends = ((0, 2), (cx - 2, 2))
+    relay(0, (None,) + tuple(range(MET, CURV)), pl.ds(MET, 6), 4)
+    climbs(ends, (1, GEO))
     wait_for(X_CHI)
-    relay(1, (CHI,), pl.ds(CHI, 1))
+    relay(1, (CHI,), pl.ds(CHI, 1), 4)
+    climbs(ends, (0, 1))
+    run(*outer, *every, False)
     wait_for(EDGE_Z)
     for at in range(4):
         packed[at + at // 2 * cx, own_y] = joined(lambda side: edge_in[side, 0, at] + edge_in[side, 1, at])
-    slopes(((0, 2), (cx - 2, 2)))
+    slopes(ends)
+    wait_for(EDGE_Y)
+    rims(ends)
     wait_for(X_GX)
-    run(*outer, *middle, False)
-    wait_for(EDGE_Y)
-    rims(((0, 2), (cx - 2, 2)))
-    run(*outer, *rim, False)
+
+    def mend(n, carry):
+        x, y = outer_x(n // tiles), lax.rem(n, tiles) * 8
+        rows = pl.ds(pl.multiple_of(y, 8), 8)
+        here = pl.ds(pl.multiple_of(TOP + y, 8), 8)
+        chi, *metric = [cells[CHI + k, x + 2, here] for k in range(GEO)]
+        gu = inverse(metric)
+        chi_part, *parts = [
+            gu[1] * first(*(slope[k, x, pl.ds(TOP + y + s, 8)] for s in (-2, -1, 1, 2))) + gu[2] * xz_two[k, x, rows]
+            for k in range(GEO)
+        ]
+        div = first(*(cells[GX, x + 2 + s, here] for s in (-2, -1, 1, 2)))
+        ham = ham_out[x, rows] + (
+            (4.0 * chi_part - chi * contract(gu, parts)) * (1.0 / 144.0) + chi * div * (1.0 / 12.0)
+        )
+        ham_out[x, rows] = ham
+        sums[0] += ham * ham
+        return carry
+
+    lax.fori_loop(0, 4 * tiles, mend, 0, unroll=2)
     wait_for(PART)
 
     def finish(n, carry):
@@ -513,7 +567,7 @@
         sums[1] += momentum[0] * momentum[0] + momentum[1] * momentum[1] + momentum[2] * momentum[2]
         return carry
 
-    lax.fori_loop(0, 4 * tiles, finish, 0, unroll=4)
+    lax.fori_loop(0, 4 * tiles, finish, 0, unroll=16)
 
     lane = lax.broadcasted_iota(jnp.int32, (8, 128), 1)
     folded = [sums[n] + pltpu.roll(sums[n], 64, 1) for n in range(2)]

time: 30.2 us -> 29.3 us (0.970)
  Pallas kernels: 29.4 us -> 28.5 us
    pallas_call x1, Pallas kernels: 28.6 us -> 27.7 us  [on_device(): pl.pallas_call(functools.partial(kernel, sizes), out_shape=(pltpu.VMEM(ch...]
where the time goes in v6:
time: 29.3 us; the launch traced here: 29.2 us
  Pallas kernels  28.5 us (97%)
  between operations  0.64 us (2%)
    pallas_call x1, Pallas kernels, on_device(): pl.pallas_call(functools.partial(kernel, sizes), out_shape=(pltpu.VMEM(ch...  27.7 us
    pallas_call x1, Pallas kernels, on_device(): pl.pallas_call(functools.partial(deliver, count), out_shape=(jax.ShapeDty...  0.82 us

profile of v6, /device:TPU:0, one launch (start us, length us, event | category | flops | bytes accessed | tf_op | source)
XLA Modules:
  0.0 29.2 jit_solution(15570987299202522667)
XLA Ops:
  0.6 27.7 %shard_map.85 = (f32[8,32,128]{2,1,0:T(8,128)S(1)}, f32[3,8,32,128]{3,2,1,0:T(8,128)S(1)}, f32[1,128]{1,0:T(1,128)S(1)}) custom-call(f32[8,32,128]{2,1,0:T(8,128)} %chi_in.1, f32[6,8,32,128]{3,2,1,0:T(8,128)} %met_in.1, f32[6,8,32,128]{3,2,1,0:T(8,128)} %curv_in.1, f32[8,32,128]{2,1,0:T(8,128)} %trk_in.1, f32[3,8,32,128]{3,2,1,0:T(8,128)} %gam_in.1, ...), custom_call_target="tpu_custom_call" | custom-call | tf_op jit(solution)/shard_map/pallas_call | solution.py:612
  28.4 0.8 %shard_map.86 = (f32[8,32,128]{2,1,0:T(8,128)}, f32[3,8,32,128]{3,2,1,0:T(8,128)}, f32[2]{0:T(128)}) custom-call(f32[8,32,128]{2,1,0:T(8,128)S(1)} %get-tuple-element.6.ham_in, f32[3,8,32,128]{3,2,1,0:T(8,128)S(1)} %get-tuple-element.7.mom_in, f32[1,128]{1,0:T(1,128)S(1)} %get-tuple-element.8.total_in), custom_call_target="tpu_custom_call" | custom-call | tf_op jit(solution)/shard_map/pallas_call | solution.py:643

commit v7 on v6

--- a/solution.py
+++ b/solution.py
@@ -558,16 +558,14 @@
     lax.fori_loop(0, 4 * tiles, mend, 0, unroll=2)
     wait_for(PART)
 
-    def finish(n, carry):
-        at, rows = n // tiles, pl.ds(pl.multiple_of(lax.rem(n, tiles) * 8, 8), 8)
+    squares = []
+    for at in range(4):
         x = outer_x(at)
-        momentum = [mom_out[i, x, rows] + part[i, at, rows] for i in range(3)]
         for i in range(3):
-            mom_out[i, x, rows] = momentum[i]
-        sums[1] += momentum[0] * momentum[0] + momentum[1] * momentum[1] + momentum[2] * momentum[2]
-        return carry
-
-    lax.fori_loop(0, 4 * tiles, finish, 0, unroll=16)
+            momentum = mom_out[i, x] + part[i, at]
+            mom_out[i, x] = momentum
+            squares += [momentum[y : y + 8] * momentum[y : y + 8] for y in range(0, cy, 8)]
+    sums[1] += total_of(squares)
 
     lane = lax.broadcasted_iota(jnp.int32, (8, 128), 1)
     folded = [sums[n] + pltpu.roll(sums[n], 64, 1) for n in range(2)]

time: 29.3 us -> 29.3 us (level)
  no operation moved by 1% of the time
where the time goes in v7:
time: 29.3 us; the launch traced here: 29.2 us
  Pallas kernels  28.5 us (97%)
  between operations  0.64 us (2%)
    pallas_call x1, Pallas kernels, on_device(): pl.pallas_call(functools.partial(kernel, sizes), out_shape=(pltpu.VMEM(ch...  27.7 us
    pallas_call x1, Pallas kernels, on_device(): pl.pallas_call(functools.partial(deliver, count), out_shape=(jax.ShapeDty...  0.82 us

profile of v7, /device:TPU:0, one launch (start us, length us, event | category | flops | bytes accessed | tf_op | source)
XLA Modules:
  0.0 29.2 jit_solution(16881962116857820120)
XLA Ops:
  0.6 27.7 %shard_map.85 = (f32[8,32,128]{2,1,0:T(8,128)S(1)}, f32[3,8,32,128]{3,2,1,0:T(8,128)S(1)}, f32[1,128]{1,0:T(1,128)S(1)}) custom-call(f32[8,32,128]{2,1,0:T(8,128)} %chi_in.1, f32[6,8,32,128]{3,2,1,0:T(8,128)} %met_in.1, f32[6,8,32,128]{3,2,1,0:T(8,128)} %curv_in.1, f32[8,32,128]{2,1,0:T(8,128)} %trk_in.1, f32[3,8,32,128]{3,2,1,0:T(8,128)} %gam_in.1, ...), custom_call_target="tpu_custom_call" | custom-call | tf_op jit(solution)/shard_map/pallas_call | solution.py:610
  28.4 0.8 %shard_map.86 = (f32[8,32,128]{2,1,0:T(8,128)}, f32[3,8,32,128]{3,2,1,0:T(8,128)}, f32[2]{0:T(128)}) custom-call(f32[8,32,128]{2,1,0:T(8,128)S(1)} %get-tuple-element.6.ham_in, f32[3,8,32,128]{3,2,1,0:T(8,128)S(1)} %get-tuple-element.7.mom_in, f32[1,128]{1,0:T(1,128)S(1)} %get-tuple-element.8.total_in), custom_call_target="tpu_custom_call" | custom-call | tf_op jit(solution)/shard_map/pallas_call | solution.py:641

commit v8 on v7

--- a/solution.py
+++ b/solution.py
@@ -12,7 +12,7 @@
 MESH = pl.DeviceIdType.MESH
 GX, CHI, MET, CURV, TRK, GY, GZ = 0, 1, 2, 8, 14, 15, 16
 GEO = 7
-X_MET, X_CHI, X_GX, Y_GEO, Y_REST, Y_PACK, Z_PACK, EDGE_Y, EDGE_Z, PART, NORM = range(11)
+X_MET, X_MET_BACK, X_CHI, X_GX, Y_GEO, Y_REST, Y_PACK, Z_PACK, EDGE_Y, EDGE_Z, PART, NORM = range(12)
 Z_FIELDS = tuple(range(CHI, GY)) + (GZ,)
 TOP = 8
 
@@ -258,7 +258,8 @@
     geo = pl.ds(CHI, GEO)
     several = nz > 2
     bulk = {
-        X_MET: cells.at[pl.ds(MET, 6), pl.ds(0, 4), own_y],
+        X_MET: cells.at[pl.ds(MET, 6), before_x, own_y],
+        X_MET_BACK: cells.at[pl.ds(MET, 6), after_x, own_y],
         X_CHI: cells.at[pl.ds(CHI, 1), pl.ds(0, 4), own_y],
         X_GX: cells.at[pl.ds(GX, 1), pl.ds(0, 4), own_y],
         Y_GEO: cells.at[geo, own_x, pl.ds(0, 4)],
@@ -287,11 +288,11 @@
             back()
             ahead()
 
-    def send_x(fields, n):
+    def send_x(fields, n, n_back=None):
         each_way(
             0,
             lambda: send(cells.at[fields, high_x, own_y], cells.at[fields, before_x, own_y], n, 0, 1),
-            lambda: send(cells.at[fields, low_x, own_y], cells.at[fields, after_x, own_y], n, 0, -1),
+            lambda: send(cells.at[fields, low_x, own_y], cells.at[fields, after_x, own_y], n if n_back is None else n_back, 0, -1),
         )
 
     def send_y(fields, n, layers=own_x):
@@ -302,7 +303,7 @@
         )
 
     loaded(0, cells.at[pl.ds(MET, 6), own_x, own_y])
-    send_x(pl.ds(MET, 6), X_MET)
+    send_x(pl.ds(MET, 6), X_MET, X_MET_BACK)
     loaded(1, cells.at[pl.ds(GX, 2), own_x, own_y])
     send_x(pl.ds(CHI, 1), X_CHI)
     send_y(geo, Y_GEO)
@@ -489,12 +490,11 @@
     rims(((2, cx - 4),))
     wait_for(Y_REST)
     run(*inner, *rim, True)
-    wait_for(X_MET)
-
-    def offer(t, carry):
-        rows = pl.ds(pl.multiple_of(TOP + t * 8, 8), 8)
-        out_rows = pl.ds(pl.multiple_of(t * 8, 8), 8)
-        for side, far, near, at, behind, sign in ((0, 0, 1, 2, 3, 1.0), (1, cx + 3, cx + 2, cx + 1, cx, -1.0)):
+
+    def offer(side, far, near, at, behind, sign):
+        def one(t, carry):
+            rows = pl.ds(pl.multiple_of(TOP + t * 8, 8), 8)
+            out_rows = pl.ds(pl.multiple_of(t * 8, 8), 8)
             edge = [cells[CURV + n, at, rows] * sign for n in range(7)]
             second_edge = [cells[CURV + n, behind, rows] * sign for n in range(7)]
             for place, slot, values in (
@@ -507,14 +507,21 @@
                     if i == 0:
                         value = value - (2.0 / 3.0) * values[6]
                     part_out[side, i, slot, out_rows] = value * (1.0 / 12.0)
-        return carry
-
-    lax.fori_loop(0, tiles, offer, 0)
-    each_way(
-        0,
-        lambda: send(part_out.at[1], part.at[:, pl.ds(0, 2)], PART, 0, 1),
-        lambda: send(part_out.at[0], part.at[:, pl.ds(2, 2)], PART, 0, -1),
-    )
+            return carry
+
+        lax.fori_loop(0, tiles, one, 0)
+
+    def offer_back():
+        wait_for(X_MET)
+        offer(0, 0, 1, 2, 3, 1.0)
+        send(part_out.at[0], part.at[:, pl.ds(2, 2)], PART, 0, -1)
+
+    def offer_ahead():
+        wait_for(X_MET_BACK)
+        offer(1, cx + 3, cx + 2, cx + 1, cx, -1.0)
+        send(part_out.at[1], part.at[:, pl.ds(0, 2)], PART, 0, 1)
+
+    each_way(0, offer_ahead, offer_back)
 
     def relay(n, fields, sliced, unroll):
         for layers in (before_x, after_x):
@@ -631,7 +638,7 @@
         ]
         + [pltpu.VMEM((GEO, cx, cy, cz), jnp.float32)] * 4
         + [pltpu.VMEM((2, cx * cy, cz), jnp.bfloat16)] * 3
-        + [pltpu.VMEM((np.prod(sizes), 128), jnp.float32), dma((4,)), dma((11,)), dma((11,))]
+        + [pltpu.VMEM((np.prod(sizes), 128), jnp.float32), dma((4,)), dma((12,)), dma((12,))]
         + [pltpu.SemaphoreType.REGULAR],
         compiler_params=pltpu.CompilerParams(
             collective_id=0, has_side_effects=True, vmem_limit_bytes=67043328 - 16 * chi_field.size - 16384

time: 29.3 us -> 29.3 us (level)
  no operation moved by 1% of the time
where the time goes in v8:
time: 29.3 us; the launch traced here: 29.2 us
  Pallas kernels  28.6 us (98%)
  between operations  0.64 us (2%)
    pallas_call x1, Pallas kernels, on_device(): pl.pallas_call(functools.partial(kernel, sizes), out_shape=(pltpu.VMEM(ch...  27.7 us
    pallas_call x1, Pallas kernels, on_device(): pl.pallas_call(functools.partial(deliver, count), out_shape=(jax.ShapeDty...  0.82 us

profile of v8, /device:TPU:0, one launch (start us, length us, event | category | flops | bytes accessed | tf_op | source)
XLA Modules:
  0.0 29.2 jit_solution(16886132962987327521)
XLA Ops:
  0.6 27.7 %shard_map.85 = (f32[8,32,128]{2,1,0:T(8,128)S(1)}, f32[3,8,32,128]{3,2,1,0:T(8,128)S(1)}, f32[1,128]{1,0:T(1,128)S(1)}) custom-call(f32[8,32,128]{2,1,0:T(8,128)} %chi_in.1, f32[6,8,32,128]{3,2,1,0:T(8,128)} %met_in.1, f32[6,8,32,128]{3,2,1,0:T(8,128)} %curv_in.1, f32[8,32,128]{2,1,0:T(8,128)} %trk_in.1, f32[3,8,32,128]{3,2,1,0:T(8,128)} %gam_in.1, ...), custom_call_target="tpu_custom_call" | custom-call | tf_op jit(solution)/shard_map/pallas_call | solution.py:617
  28.4 0.8 %shard_map.86 = (f32[8,32,128]{2,1,0:T(8,128)}, f32[3,8,32,128]{3,2,1,0:T(8,128)}, f32[2]{0:T(128)}) custom-call(f32[8,32,128]{2,1,0:T(8,128)S(1)} %get-tuple-element.6.ham_in, f32[3,8,32,128]{3,2,1,0:T(8,128)S(1)} %get-tuple-element.7.mom_in, f32[1,128]{1,0:T(1,128)S(1)} %get-tuple-element.8.total_in), custom_call_target="tpu_custom_call" | custom-call | tf_op jit(solution)/shard_map/pallas_call | solution.py:648

commit v9 on v7

--- a/solution.py
+++ b/solution.py
@@ -556,6 +556,13 @@
         return carry
 
     lax.fori_loop(0, 4 * tiles, mend, 0, unroll=2)
+    lane = lax.broadcasted_iota(jnp.int32, (8, 128), 1)
+
+    def folded(value):
+        return value + pltpu.roll(value, 64, 1)
+
+    ham_sum = jnp.where(lane < 64, folded(sums[0]), 0.0)
+    pl.semaphore_wait(ready, ny * nz - 1)
     wait_for(PART)
 
     squares = []
@@ -565,12 +572,9 @@
             momentum = mom_out[i, x] + part[i, at]
             mom_out[i, x] = momentum
             squares += [momentum[y : y + 8] * momentum[y : y + 8] for y in range(0, cy, 8)]
-    sums[1] += total_of(squares)
-
-    lane = lax.broadcasted_iota(jnp.int32, (8, 128), 1)
-    folded = [sums[n] + pltpu.roll(sums[n], 64, 1) for n in range(2)]
-    total = jnp.sum(jnp.where(lane < 64, folded[0], folded[1]), axis=0, keepdims=True)
-    pl.semaphore_wait(ready, ny * nz - 1)
+
+    mom_sum = folded(sums[1] + total_of(squares))
+    total = jnp.sum(jnp.where(lane < 64, ham_sum, mom_sum), axis=0, keepdims=True)
     axes = (0, 1, 2)
     here = pl.ds(place_in(axes), 1)
     slots[here] = total

time: 29.3 us -> 29.3 us (level)
  no operation moved by 1% of the time
where the time goes in v9:
time: 29.3 us; the launch traced here: 29.2 us
  Pallas kernels  28.5 us (97%)
  between operations  0.64 us (2%)
    pallas_call x1, Pallas kernels, on_device(): pl.pallas_call(functools.partial(kernel, sizes), out_shape=(pltpu.VMEM(ch...  27.7 us
    pallas_call x1, Pallas kernels, on_device(): pl.pallas_call(functools.partial(deliver, count), out_shape=(jax.ShapeDty...  0.82 us

profile of v9, /device:TPU:0, one launch (start us, length us, event | category | flops | bytes accessed | tf_op | source)
XLA Modules:
  0.0 29.2 jit_solution(15067011892841052727)
XLA Ops:
  0.6 27.7 %shard_map.85 = (f32[8,32,128]{2,1,0:T(8,128)S(1)}, f32[3,8,32,128]{3,2,1,0:T(8,128)S(1)}, f32[1,128]{1,0:T(1,128)S(1)}) custom-call(f32[8,32,128]{2,1,0:T(8,128)} %chi_in.1, f32[6,8,32,128]{3,2,1,0:T(8,128)} %met_in.1, f32[6,8,32,128]{3,2,1,0:T(8,128)} %curv_in.1, f32[8,32,128]{2,1,0:T(8,128)} %trk_in.1, f32[3,8,32,128]{3,2,1,0:T(8,128)} %gam_in.1, ...), custom_call_target="tpu_custom_call" | custom-call | tf_op jit(solution)/shard_map/pallas_call | solution.py:614
  28.4 0.8 %shard_map.86 = (f32[8,32,128]{2,1,0:T(8,128)}, f32[3,8,32,128]{3,2,1,0:T(8,128)}, f32[2]{0:T(128)}) custom-call(f32[8,32,128]{2,1,0:T(8,128)S(1)} %get-tuple-element.6.ham_in, f32[3,8,32,128]{3,2,1,0:T(8,128)S(1)} %get-tuple-element.7.mom_in, f32[1,128]{1,0:T(1,128)S(1)} %get-tuple-element.8.total_in), custom_call_target="tpu_custom_call" | custom-call | tf_op jit(solution)/shard_map/pallas_call | solution.py:645
